TPU v7x, 128 devices: a whole 4x4x4 slice. The times are simulated.
128 devices in a mesh: row: 16 (over y, z), col: 8 (over x, core).
Axes of the slice: x: 4, y: 4, z: 4, core: 2. Of those that a mesh axis runs over, the one named last changes fastest.
Arguments:
- features: bfloat16 [32768, 512], P(('col', 'row')), may hold values from -6 to 6
- blocks: bfloat16 [16, 8, 48, 128, 128], P('row', 'col'), may hold values from -0.375 to 0.375
- block_rows: int32 [16, 8, 48], P('row', 'col'), may hold values from 0 to 15, as said below
- block_cols: int32 [16, 8, 48], P('row', 'col'), may hold values from 0 to 31, as said below
- block_count: int32 [16, 8], P('row', 'col'), may hold values from 8 to 48, as said below
- weight: bfloat16 [512, 512], replicated, may hold values from -0.25 to 0.25
- bias_vector: float32 [512], replicated, may hold values from -4 to 4
- upstream: bfloat16 [32768, 512], P(('row', 'col')), may hold values from -6 to 6
Outputs:
- activated: bfloat16 [32768, 512], P(('row', 'col'))
- grad_weight: float32 [512, 512], replicated
- grad_bias: float32 [512], replicated
- grad_features: bfloat16 [32768, 512], P(('col', 'row'))
Inputs may be any that keep to these rules, and one draw needn't show every extreme that they name: `block_rows`: the live (block row, block column) pairs of one device are distinct. `block_cols`: paired slot by slot with block_rows. `block_count`: live slots come first; some device has exactly 48 live slots.
All inputs are finite; a program needn't handle non-finite values.
Results may differ from a plain program's by a relative error of at most 0.0061.
Values may be sent and summed in bfloat16 or wider, within the bound.
A program may use at most 64 MiB of HBM per device.

v0:
```python
import math

import jax
import jax.numpy as jnp
from jax import lax
from jax.sharding import PartitionSpec as P


def block_product(block_tiles, take_index, put_index, live_count, source, out_rows, transposed):
    slot_total = block_tiles.shape[0]
    block_size = block_tiles.shape[1]
    width = source.shape[1]
    group_size = math.gcd(slot_total, 32)
    source_blocks = source.reshape(-1, block_size, width)
    totals = jnp.zeros((out_rows // block_size, block_size, width), jnp.float32)
    form = "gji,gjh->gih" if transposed else "gij,gjh->gih"

    def one_turn(turn, totals):
        first_slot = turn * group_size
        chosen = lax.dynamic_slice_in_dim(block_tiles, first_slot, group_size, 0)
        take_now = lax.dynamic_slice_in_dim(take_index, first_slot, group_size, 0)
        put_now = lax.dynamic_slice_in_dim(put_index, first_slot, group_size, 0)
        live_mask = first_slot + jnp.arange(group_size, dtype=jnp.int32) < live_count
        chosen = jnp.where(live_mask[:, None, None], chosen, jnp.zeros_like(chosen))
        picked = source_blocks[take_now]
        product = jnp.einsum(form, chosen, picked, preferred_element_type=jnp.float32)
        return totals.at[put_now].add(product)

    last_turn = slot_total // group_size
    totals = lax.fori_loop(0, last_turn, one_turn, totals)
    return totals.reshape(out_rows, width)


def dense_part(hidden, weight, bias_vector, upstream):
    preact = jnp.dot(hidden, weight, preferred_element_type=jnp.float32) + bias_vector
    sigmoid_pre = jax.nn.sigmoid(preact)
    activated = (preact * sigmoid_pre).astype(jnp.bfloat16)
    dpre = (
        upstream.astype(jnp.float32) * sigmoid_pre * (1.0 + preact * (1.0 - sigmoid_pre))
    ).astype(jnp.bfloat16)
    grad_weight = lax.dot_general(
        hidden, dpre, (((0,), (0,)), ((), ())), preferred_element_type=jnp.float32
    )
    grad_bias = jnp.sum(dpre.astype(jnp.float32), axis=0)
    dhidden = lax.dot_general(
        dpre, weight, (((1,), (1,)), ((), ())), preferred_element_type=jnp.float32
    ).astype(jnp.bfloat16)
    return (activated, grad_weight, grad_bias, dhidden)


def shards(features, blocks, block_rows, block_cols, block_count, weight, bias_vector, upstream):
    node_dev = features.shape[0]
    row_size = lax.axis_size("row")
    col_size = lax.axis_size("col")
    node_total = node_dev * row_size * col_size
    scale_factor = 1.0 / math.sqrt(node_total)
    block_tiles = blocks[0, 0]
    rows_local = block_rows[0, 0]
    cols_local = block_cols[0, 0]
    live_count = block_count[0, 0]
    gathered = lax.all_gather(features, "row", axis=0, tiled=True)
    partial_value = block_product(
        block_tiles, cols_local, rows_local, live_count, gathered, node_dev * col_size, False
    )
    hidden = lax.psum_scatter(partial_value, "col", scatter_dimension=0, tiled=True).astype(
        jnp.bfloat16
    )
    activated, grad_weight, grad_bias, dhidden = dense_part(hidden, weight, bias_vector, upstream)
    grad_weight, grad_bias = lax.psum((grad_weight, grad_bias), ("row", "col"))
    dhidden_rows = lax.all_gather(dhidden, "col", axis=0, tiled=True)
    grad_weight = grad_weight * scale_factor
    grad_bias = grad_bias * scale_factor
    grad_partial = block_product(
        block_tiles, rows_local, cols_local, live_count, dhidden_rows, node_dev * row_size, True
    )
    grad_features = lax.psum_scatter(grad_partial, "row", scatter_dimension=0, tiled=True).astype(
        jnp.bfloat16
    )
    return (activated, grad_weight, grad_bias, grad_features)


def solution(mesh):
    in_specs = (
        P(("col", "row"), None),
        P("row", "col", None, None, None),
        P("row", "col", None),
        P("row", "col", None),
        P("row", "col"),
        P(),
        P(),
        P(("row", "col"), None),
    )
    out_specs = (P(("row", "col"), None), P(), P(), P(("col", "row"), None))
    return jax.shard_map(shards, mesh=mesh, in_specs=in_specs, out_specs=out_specs, check_vma=False)
```

profile of v0, /device:TPU:0, one launch (start us, length us, event | category | flops | bytes accessed | tf_op | source)
XLA Modules:
  0.0 432.3 jit_solution(1796338669896507665)
XLA Ops:
  8.0 56.2 %all-gather.3.cloned.1.call-done = bf16[4096,512]{1,0:T(8,128)(2,1)} async-done(((bf16[256,512]{1,0:T(8,128)(2,1)}), bf16[4096,512]{1,0:T(8,128)(2,1)}) %all-gather.3.cloned.1.call-update) | async-done | bytes 4194320 | tf_op jit(solution)/shard_map/all_gather | solution.py:61
  66.7 49.7 %while.26 = (s32[]{:T(128)}, f32[16,128,512]{2,1,0:T(8,128)}, s32[48]{0:T(128)S(1)}, s32[]{:T(128)}, bf16[48,128,128]{2,1,0:T(8,128)(2,1)}, /*index=5*/s32[48]{0...) while((s32[]{:T(128)}, f32[16,128,512]{2,1,0:T(8,128)}, ...), condition=%wide.region_2.3_spmd, body=%wide.region_0.2_spmd.sunk | while | flops 269747328 | bytes 23597708 | solution.py:30
  67.4 2.9 gather_fusion
  70.3 3.8 fusion.31
  74.1 9.1 %scatter_fusion = f32[16,128,512]{2,1,0:T(8,128)} fusion(f32[16,128,512]{2,1,0:T(8,128)} %get-tuple-element.402, s32[16]{0:T(128)S(1)} %get-tuple-element.379, f32[16,128,512]{2,1,0:T(8,128)} %fusion.31), kind=kCustom, calls=%fused_computation.2.clone.1 | custom fusion | flops 1048576 | bytes 12582976 | tf_op jit(solution)/shard_map/while/body/eval_jaxpr/scatter-add | solution.py:27
  84.0 2.9 gather_fusion
  86.9 3.8 fusion.31
  90.6 9.2 %scatter_fusion = f32[16,128,512]{2,1,0:T(8,128)} fusion(f32[16,128,512]{2,1,0:T(8,128)} %get-tuple-element.402, s32[16]{0:T(128)S(1)} %get-tuple-element.379, f32[16,128,512]{2,1,0:T(8,128)} %fusion.31), kind=kCustom, calls=%fused_computation.2.clone.1 | custom fusion | flops 1048576 | bytes 12582976 | tf_op jit(solution)/shard_map/while/body/eval_jaxpr/scatter-add | solution.py:27
  100.6 2.9 gather_fusion
  103.5 3.8 fusion.31
  107.3 9.1 %scatter_fusion = f32[16,128,512]{2,1,0:T(8,128)} fusion(f32[16,128,512]{2,1,0:T(8,128)} %get-tuple-element.402, s32[16]{0:T(128)S(1)} %get-tuple-element.379, f32[16,128,512]{2,1,0:T(8,128)} %fusion.31), kind=kCustom, calls=%fused_computation.2.clone.1 | custom fusion | flops 1048576 | bytes 12582976 | tf_op jit(solution)/shard_map/while/body/eval_jaxpr/scatter-add | solution.py:27
  116.5 37.9 %reduce-scatter.3.cloned.1.call-done = f32[256,512]{1,0:T(8,128)} async-done(((f32[2048,512]{1,0:T(8,128)}), f32[256,512]{1,0:T(8,128)}) %reduce-scatter.3.cloned.1.call-update) | async-done | bytes 524304 | tf_op jit(solution)/shard_map/reduce_scatter | solution.py:65
  160.8 21.3 %all-gather.5.cloned.1.call-done = bf16[2048,512]{1,0:T(8,128)(2,1)} async-done(((bf16[256,512]{1,0:T(8,128)(2,1)}), bf16[2048,512]{1,0:T(8,128)(2,1)}) %all-gather.5.cloned.1.call-update) | async-done | bytes 2097168 | tf_op jit(solution)/shard_map/all_gather | solution.py:70
  182.1 4.3 broadcast_in_dim.75
  186.4 49.4 %while.27 = (s32[]{:T(128)}, f32[32,128,512]{2,1,0:T(8,128)}, s32[48]{0:T(128)S(1)}, s32[]{:T(128)}, bf16[48,128,128]{1,2,0:T(8,128)(2,1)}, /*index=5*/s32[48]{0...) while((s32[]{:T(128)}, f32[32,128,512]{2,1,0:T(8,128)}, ...), condition=%wide.region_9.10_spmd, body=%wide.region_7.9_spmd.sunk | while | flops 269747328 | bytes 23597708 | solution.py:30
  189.4 3.8 fusion.34
  193.2 9.7 %scatter_fusion.1 = f32[32,128,512]{2,1,0:T(8,128)} fusion(f32[32,128,512]{2,1,0:T(8,128)} %get-tuple-element.435, s32[16]{0:T(128)S(1)} %get-tuple-element.388, f32[16,128,512]{2,1,0:T(8,128)} %fusion.34), kind=kCustom, calls=%fused_computation.3.clone.1 | custom fusion | flops 1048576 | bytes 12582976 | tf_op jit(solution)/shard_map/while/body/eval_jaxpr/scatter-add | solution.py:27
  205.9 3.8 fusion.34
  209.7 9.6 %scatter_fusion.1 = f32[32,128,512]{2,1,0:T(8,128)} fusion(f32[32,128,512]{2,1,0:T(8,128)} %get-tuple-element.435, s32[16]{0:T(128)S(1)} %get-tuple-element.388, f32[16,128,512]{2,1,0:T(8,128)} %fusion.34), kind=kCustom, calls=%fused_computation.3.clone.1 | custom fusion | flops 1048576 | bytes 12582976 | tf_op jit(solution)/shard_map/while/body/eval_jaxpr/scatter-add | solution.py:27
  222.3 3.8 fusion.34
  226.1 9.7 %scatter_fusion.1 = f32[32,128,512]{2,1,0:T(8,128)} fusion(f32[32,128,512]{2,1,0:T(8,128)} %get-tuple-element.435, s32[16]{0:T(128)S(1)} %get-tuple-element.388, f32[16,128,512]{2,1,0:T(8,128)} %fusion.34), kind=kCustom, calls=%fused_computation.3.clone.1 | custom fusion | flops 1048576 | bytes 12582976 | tf_op jit(solution)/shard_map/while/body/eval_jaxpr/scatter-add | solution.py:27
  235.8 66.8 %psum.15 = f32[512]{0:T(512)S(1)} all-reduce(f32[512]{0:T(512)S(1)} %get-tuple-element.289), channel_id=1, replica_groups=mesh['row'=16,'col'=8] {'row','col'}, use_global_device_ids=true, to_apply=%region_6.7 | all-reduce | flops 512 | bytes 4096 | tf_op jit(solution)/shard_map/psum | solution.py:69
  303.2 32.1 %all-reduce.2.cloned.1.call-done = f32[512,512]{1,0:T(8,128)} async-done(((f32[512,512]{1,0:T(8,128)}), f32[512,512]{1,0:T(8,128)}) %all-reduce.2.cloned.1.call-update) | async-done | bytes 1048592 | tf_op jit(solution)/shard_map/psum | solution.py:69
  337.6 86.4 %reduce-scatter.5.cloned.1.call-done = f32[256,512]{1,0:T(8,128)} async-done(((f32[4096,512]{1,0:T(8,128)}), f32[256,512]{1,0:T(8,128)}) %reduce-scatter.5.cloned.1.call-update) | async-done | bytes 524304 | tf_op jit(solution)/shard_map/reduce_scatter | solution.py:76
  (53 shorter events, 25.7 us)
Async XLA Ops:
  7.2 147.2 %copy-start = (bf16[512,512]{1,0:T(8,128)(2,1)S(1)}, bf16[512,512]{1,0:T(8,128)(2,1)}, u32[]{:S(2)}) copy-start(bf16[512,512]{1,0:T(8,128)(2,1)} %param.17) | copy-start | bytes 1572868
  7.2 59.5 %copy-start.4 = (s32[1,1,48]{2,1,0:T(1,128)S(1)}, s32[1,1,48]{2,1,0:T(1,128)}, u32[]{:S(2)}) copy-start(s32[1,1,48]{2,1,0:T(1,128)} %param.15) | copy-start | bytes 580
  7.2 59.5 %copy-start.3 = (s32[1,1,48]{2,1,0:T(1,128)S(1)}, s32[1,1,48]{2,1,0:T(1,128)}, u32[]{:S(2)}) copy-start(s32[1,1,48]{2,1,0:T(1,128)} %param.14) | copy-start | bytes 580
  7.2 57.0 %all-gather.3.cloned.1.call-start = ((), (), s32[]{:S(2)}) async-start(), calls=%async_computation.2 | async-start | bytes 4456448 | tf_op jit(solution)/shard_map/all_gather | solution.py:61
  7.9 146.5 %reduce-scatter.3.cloned.1.call-start = ((), (), s32[]{:S(2)}) async-start(), calls=%async_computation.3 | async-start | bytes 4718592 | tf_op jit(solution)/shard_map/reduce_scatter | solution.py:65
  116.4 38.0 %copy-start.5 = (bf16[256,512]{1,0:T(8,128)(2,1)S(1)}, bf16[256,512]{1,0:T(8,128)(2,1)}, u32[]{:S(2)}) copy-start(bf16[256,512]{1,0:T(8,128)(2,1)} %param.19) | copy-start | bytes 786436
  116.4 38.0 %copy-start.6 = (f32[512]{0:T(512)S(1)}, f32[512]{0:T(512)}, u32[]{:S(2)}) copy-start(f32[512]{0:T(512)} %param.18) | copy-start | bytes 6148
  116.4 41.4 %copy-start.1 = (bf16[48,128,128]{2,1,0:T(8,128)(2,1)S(1)}, bf16[48,128,128]{2,1,0:T(8,128)(2,1)}, u32[]{:S(2)}) copy-start(bf16[48,128,128]{2,1,0:T(8,128)(2,1)} %get-tuple-element.467) | copy-start | bytes 4718596
  116.4 65.7 %all-gather.5.cloned.1.call-start = ((), (), s32[]{:S(2)}) async-start(), calls=%async_computation.5 | async-start | bytes 2359296 | tf_op jit(solution)/shard_map/all_gather | solution.py:70
  154.4 5.0 %copy-start.2 = (f32[256,512]{1,0:T(8,128)S(1)}, f32[256,512]{1,0:T(8,128)}, u32[]{:S(2)}) copy-start(f32[256,512]{1,0:T(8,128)} %reduce-scatter.3.cloned.1.call-done) | copy-start | bytes 1572868
  157.8 177.5 %all-reduce.2.cloned.1.call-start = ((), (), s32[]{:S(2)}) async-start(), calls=%async_computation.4 | async-start | bytes 2097152 | tf_op jit(solution)/shard_map/psum | solution.py:69
  160.8 263.2 %reduce-scatter.5.cloned.1.call-start = ((), (), s32[]{:S(2)}) async-start(), calls=%async_computation.6 | async-start | bytes 8912896 | tf_op jit(solution)/shard_map/reduce_scatter | solution.py:76
Sparse Core Ops, SparseCore 0:
  10.1 53.9 all-gather.2
  116.6 37.7 reduce-scatter.2
  157.9 24.1 all-gather.4
  187.3 147.9 all-reduce.1
  338.6 85.3 reduce-scatter.4
where the time goes:
time: 433 us; the launch traced here: 432 us
  waiting for transfers between devices  235 us (54%)
  blocking collectives  66.8 us (15%)
  other arithmetic  65.6 us (15%)
  matrix products  27.3 us (6%)
  local copies, waits for them, and re-layouts  23.9 us (6%)
  between operations  13.8 us (3%)
    reduce_scatter x1, waiting for transfers between devices, shards(): lax.psum_scatter(grad_partial, 'row', scatter_dimension=0, tiled=True)  86.4 us
    psum x1, blocking collectives, shards(): grad_weight, grad_bias = lax.psum((grad_weight, grad_bias), ('row', 'col'))  66.8 us
    scatter-add x6, other arithmetic, one_turn(): return totals.at[put_now].add(product)  56.5 us
    all_gather x1, waiting for transfers between devices, shards(): gathered = lax.all_gather(features, 'row', axis=0, tiled=True)  56.2 us
    reduce_scatter x1, waiting for transfers between devices, shards(): lax.psum_scatter(partial_value, 'col', scatter_dimension=0, tiled=True)  37.9 us
    psum x1, waiting for transfers between devices, shards(): grad_weight, grad_bias = lax.psum((grad_weight, grad_bias), ('row', 'col'))  32.1 us
    dot_general x6, matrix products, one_turn(): jnp.einsum(form, chosen, picked, preferred_element_type=jnp.float32)  22.6 us
    all_gather x1, waiting for transfers between devices, shards(): dhidden_rows = lax.all_gather(dhidden, 'col', axis=0, tiled=True)  21.3 us
  transfers between devices with their start and end apart: 5, of which 5 were waited for; matrix products, arithmetic and copies ran while one was open for 14% of the time, Pallas kernels for 0%

commit v1 on v0

v1 whole, which is shorter than its diff:
```python
import functools
import math

import jax
import jax.numpy as jnp
from jax import lax
from jax.experimental import pallas as pl
from jax.experimental.pallas import tpu as pltpu
from jax.sharding import PartitionSpec as P

MESH = pl.DeviceIdType.MESH
F32 = jnp.float32
BF16 = jnp.bfloat16
SIDE = 4
TILE = 128
WIDE = 256
CHUNKS = 2
KBLOCKS = 32
IBLOCKS = 16
SLOTS = 48
GATHER_MESSAGES = 60
MESSAGES = 168


def wrap(value):
    return value % SIDE


def at_k(h, a, b):
    a, b = wrap(a), wrap(b)
    dy, dz = (a, b) if h == 0 else (b, a)
    return (dy * SIDE + dz) * 2 + h


def step_kernel(
    scale,
    tbl,
    feat,
    blocks,
    weight,
    bias,
    ups,
    act_o,
    gf_o,
    gw_o,
    gb_o,
    G,
    BK,
    BT,
    WT,
    UP,
    PS,
    S1,
    R0,
    XS,
    XR,
    HD,
    DP,
    DG,
    TK,
    UK,
    SB,
    SR,
    GP,
    AK,
    AX,
    AXR,
    AY,
    AYR,
    AZ,
    AZR,
    FK,
    lsem,
    ssem,
    rsem,
):
    ri = lax.axis_index("row")
    ci = lax.axis_index("col")
    y, z = ri // SIDE, ri % SIDE
    x, k = ci // 2, ci % 2
    turn = 1 - 2 * k

    def dev(dy=0, dz=0, dx=0, dk=0):
        row = ((y + dy + SIDE) % SIDE) * SIDE + (z + dz + SIDE) % SIDE
        col = ((x + dx + SIDE) % SIDE) * 2 + (k + dk) % 2
        return (row, col)

    def along(h, first, step):
        if (h == 0) == first:
            return dev(dy=step)
        return dev(dz=step)

    messages = {}

    def send(key, src, dst, to, landing=None):
        number = len(messages)
        copy = pltpu.make_async_remote_copy(
            src_ref=src,
            dst_ref=dst,
            send_sem=ssem.at[number],
            recv_sem=rsem.at[number],
            device_id=to,
            device_id_type=MESH,
        )
        copy.start()
        if landing is not None:
            copy_in = pltpu.make_async_remote_copy(
                src_ref=landing,
                dst_ref=landing,
                send_sem=ssem.at[number],
                recv_sem=rsem.at[number],
                device_id=to,
                device_id_type=MESH,
            )
        else:
            copy_in = copy
        messages[key] = (copy, copy_in)

    def take(key):
        messages[key][1].wait_recv()

    local = []

    def fetch(src, dst):
        copy = pltpu.make_async_copy(src, dst, lsem.at[len(local)])
        copy.start()
        local.append(copy)
        return copy

    own = [
        [
            fetch(
                feat.at[pl.ds(h * TILE, TILE), pl.ds(c * WIDE, WIDE)],
                G.at[c, at_k(h, 0, 0)],
            )
            for h in range(2)
        ]
        for c in range(CHUNKS)
    ]
    blocks_in = fetch(blocks, BK.at[pl.ds(0, SLOTS)])
    weight_in = fetch(weight, WT)
    ups_in = fetch(ups, UP)

    barrier = pltpu.get_barrier_semaphore()
    partners = [dev(dk=1)]
    for step in (1, -1, 2):
        partners += [dev(dy=step), dev(dz=step), dev(dx=step)]
    for partner in partners:
        pl.semaphore_signal(barrier, inc=1, device_id=partner, device_id_type=MESH)
    BK[SLOTS] = jnp.zeros((TILE, TILE), BF16)
    BT[SLOTS] = jnp.zeros((TILE, TILE), BF16)
    pl.semaphore_wait(barrier, len(partners))

    def first_way(c):
        return 1 if c == 0 else -1

    def second_way(a):
        return 1 if a in (0, 1) else -1

    def second_sends(c, h, a):
        src = G.at[c, at_k(h, a, 0)]
        send(("g2p", c, h, a), src, G.at[c, at_k(h, a, -1)], along(h, False, 1))
        send(("g2m", c, h, a), src, G.at[c, at_k(h, a, 1)], along(h, False, -1))

    def gather_0(c):
        for h in range(2):
            own[c][h].wait()
        for h in range(2):
            src = G.at[c, at_k(h, 0, 0)]
            send(("g1p", c, h), src, G.at[c, at_k(h, -1, 0)], along(h, True, 1))
            send(("g1m", c, h), src, G.at[c, at_k(h, 1, 0)], along(h, True, -1))
        for h in range(2):
            second_sends(c, h, 0)

    def gather_1(c):
        e = first_way(c)
        for h in range(2):
            take(("g1p" if e == 1 else "g1m", c, h))
            send(
                ("g1r", c, h),
                G.at[c, at_k(h, -e, 0)],
                G.at[c, at_k(h, 2, 0)],
                along(h, True, e),
            )
            second_sends(c, h, -e)
        for h in range(2):
            take(("g1m" if e == 1 else "g1p", c, h))
            second_sends(c, h, e)

    def second_relay(c, h, a):
        e = second_way(a)
        take(("g2p" if e == 1 else "g2m", c, h, a))
        send(
            ("g2r", c, h, a),
            G.at[c, at_k(h, a, -e)],
            G.at[c, at_k(h, a, 2)],
            along(h, False, e),
        )

    def second_other(c, h, a):
        e = second_way(a)
        take(("g2m" if e == 1 else "g2p", c, h, a))

    def gather_2(c):
        for h in range(2):
            second_relay(c, h, 0)
        for h in range(2):
            second_other(c, h, 0)

    def gather_3(c):
        for h in range(2):
            take(("g1r", c, h))
            second_sends(c, h, 2)

    def gather_4(c):
        for a in (1, -1):
            for h in range(2):
                second_relay(c, h, a)
        for a in (1, -1):
            for h in range(2):
                second_other(c, h, a)

    def gather_5(c):
        for h in range(2):
            take(("g2r", c, h, 0))

    def gather_6(c):
        for h in range(2):
            second_relay(c, h, 2)
        for h in range(2):
            second_other(c, h, 2)

    def gather_7(c):
        for a in (1, -1):
            for h in range(2):
                take(("g2r", c, h, a))

    def gather_8(c):
        for h in range(2):
            take(("g2r", c, h, 2))

    rows_at_once = 4
    turns = IBLOCKS // rows_at_once

    def multiply(c, ks, first=False):
        @pl.loop(0, turns)
        def _(m):
            lhs = jnp.concatenate(
                [
                    jnp.concatenate(
                        [BK[tbl[kk * IBLOCKS + m * rows_at_once + j]] for kk in ks],
                        axis=1,
                    )
                    for j in range(rows_at_once)
                ],
                axis=0,
            )
            rhs = jnp.concatenate([G[c, kk] for kk in ks], axis=0)
            value = jnp.dot(lhs, rhs, preferred_element_type=F32)
            if not first:
                value = value + PS[c, m]
            PS[c, m] = value

    def halves(pairs):
        return [at_k(h, a, b) for a, b in pairs for h in range(2)]

    def multiply_own(c):
        multiply(c, halves([(0, 0)]), first=True)

    def multiply_1(c):
        multiply(c, halves([(1, 0), (-1, 0)]))

    def multiply_2(c):
        multiply(c, halves([(0, 1), (0, -1)]))

    def multiply_35(c):
        multiply(c, halves([(2, 0), (0, 2)]))

    def multiply_4(c):
        multiply(c, halves([(1, 1), (1, -1)]))
        multiply(c, halves([(-1, 1), (-1, -1)]))

    def multiply_6(c):
        multiply(c, halves([(2, 1), (2, -1)]))

    def multiply_7(c):
        multiply(c, halves([(1, 2), (-1, 2)]))

    def multiply_8(c):
        multiply(c, halves([(2, 2)]))

    def part_of(c, dk, dx):
        place = dk * SIDE + dx
        return PS[c, place // 2, pl.ds((place % 2) * 256, 256), :]

    def reduce_0(c):
        for dx in (2, 3, 1, 0):
            S1[c, dx] = part_of(c, 1, dx).astype(BF16)
            mirrored = wrap(-dx)
            send(("c0", c, mirrored), S1.at[c, dx], R0.at[c, mirrored], dev(dk=1))

    def paired(c, dx):
        take(("c0", c, dx))
        return part_of(c, 0, dx) + R0[c, dx].astype(F32)

    def reduce_1(c):
        XS[c, 0] = paired(c, 2).astype(BF16)
        send(("cf", c), XS.at[c, 0], XR.at[c, 0], dev(dx=turn))
        XS[c, 1] = paired(c, 3).astype(BF16)
        send(("cd", c), XS.at[c, 1], XR.at[c, 1], dev(dx=-turn))

    def reduce_2(c):
        value = paired(c, 1)
        take(("cf", c))
        XS[c, 2] = (value + XR[c, 0].astype(F32)).astype(BF16)
        send(("cr", c), XS.at[c, 2], XR.at[c, 2], dev(dx=turn))

    def reduce_3(c):
        value = paired(c, 0)
        take(("cd", c))
        value = value + XR[c, 1].astype(F32)
        take(("cr", c))
        value = value + XR[c, 2].astype(F32)
        HD[:, c * WIDE : (c + 1) * WIDE] = value.astype(BF16)

    def turn_blocks():
        @pl.loop(0, SLOTS)
        def _(s):
            BT[s] = BK[s].T

    gather_0(0)
    blocks_in.wait()
    multiply_own(0)
    gather_1(0)
    multiply_1(0)
    gather_0(1)
    gather_2(0)
    multiply_2(0)
    gather_3(0)
    multiply_own(1)
    gather_4(0)
    multiply_4(0)
    gather_1(1)
    gather_5(0)
    multiply_35(0)
    gather_6(0)
    gather_2(1)
    multiply_6(0)
    gather_7(0)
    multiply_7(0)
    gather_8(0)
    gather_3(1)
    multiply_8(0)
    reduce_0(0)
    multiply_1(1)
    reduce_1(0)
    gather_4(1)
    multiply_2(1)
    reduce_2(0)
    gather_5(1)
    multiply_35(1)
    gather_6(1)
    multiply_4(1)
    reduce_3(0)
    multiply_6(1)
    gather_7(1)
    multiply_7(1)
    gather_8(1)
    multiply_8(1)
    reduce_0(1)
    reduce_1(1)
    turn_blocks()
    reduce_2(1)
    weight_in.wait()
    ups_in.wait()
    reduce_3(1)

    bias_rows = []
    for n in range(CHUNKS):
        columns = slice(n * WIDE, (n + 1) * WIDE)
        pre = jnp.dot(HD[...], WT[:, columns], preferred_element_type=F32) + bias[:, columns]
        sig = jax.nn.sigmoid(pre)
        act_o[:, columns] = (pre * sig).astype(BF16)
        dpre = (UP[:, columns].astype(F32) * sig * (1.0 + pre * (1.0 - sig))).astype(BF16)
        DP[:, columns] = dpre
        bias_rows.append(jnp.sum(dpre.astype(F32).reshape(32, 8, WIDE), axis=0))

    def spread_0(c):
        value = lax.dot_general(
            DP[...],
            WT[pl.ds(c * WIDE, WIDE), :],
            (((1,), (1,)), ((), ())),
            preferred_element_type=F32,
        )
        DG[c, 0] = value.astype(BF16)
        send(("sp", c), DG.at[c, 0], DG.at[c, 3], dev(dx=turn))
        send(("sm", c), DG.at[c, 0], DG.at[c, 1], dev(dx=-turn))
        send(("sc", c, 0), DG.at[c, 0], DG.at[c, SIDE], dev(dk=1))

    def spread_1(c):
        take(("sp", c))
        send(("sr", c), DG.at[c, 3], DG.at[c, 2], dev(dx=turn))
        send(("sc", c, 1), DG.at[c, 3], DG.at[c, SIDE + 1], dev(dk=1))
        take(("sm", c))
        send(("sc", c, 2), DG.at[c, 1], DG.at[c, SIDE + 3], dev(dk=1))

    def spread_2(c):
        take(("sr", c))
        send(("sc", c, 3), DG.at[c, 2], DG.at[c, SIDE + 2], dev(dk=1))

    def spread_3(c):
        for n in range(SIDE):
            take(("sc", c, n))

    def weight_0():
        value = lax.dot_general(
            HD[...], DP[...], (((0,), (0,)), ((), ())), preferred_element_type=F32
        )
        GP[..., 0:16, :] = value.reshape(2, SIDE, SIDE, 16, 512)
        for n in range(CHUNKS):
            GP[..., 16:24, n * WIDE : (n + 1) * WIDE] = jnp.broadcast_to(
                bias_rows[n], (2, SIDE, SIDE, 8, WIDE)
            )
        send(("wk",), GP.at[1 - k], AK, dev(dk=1))

    def weight_1():
        take(("wk",))
        AX[...] = GP[k] + AK[...]
        for n in (2, 1, 3):
            send(("wx", n), AX.at[(x + n) % SIDE], AXR.at[n - 1], dev(dx=n))

    def weight_2():
        value = AX[x]
        for n in (2, 1, 3):
            take(("wx", n))
            value = value + AXR[n - 1]
        AY[...] = value
        for n in (2, 1, 3):
            send(("wy", n), AY.at[(y + n) % SIDE], AYR.at[n - 1], dev(dy=n))

    def weight_3():
        value = AY[y]
        for n in (2, 1, 3):
            take(("wy", n))
            value = value + AYR[n - 1]
        for n in range(SIDE):
            AZ[n] = value[:, n * TILE : (n + 1) * TILE]
        for n in (2, 1, 3):
            send(("wz", n), AZ.at[(z + n) % SIDE], AZR.at[n - 1], dev(dz=n))

    def weight_4():
        value = AZ[z]
        for n in (2, 1, 3):
            take(("wz", n))
            value = value + AZR[n - 1]
        FK[k, x, y, z] = value * scale
        mine = FK.at[k, x, y, z]
        for n in (2, 1, 3):
            send(("vz", n), mine, mine, dev(dz=n), FK.at[k, x, y, (z + SIDE - n) % SIDE])

    def weight_5():
        for n in (2, 1, 3):
            take(("vz", n))
        mine = FK.at[k, x, y]
        for n in (2, 1, 3):
            send(("vy", n), mine, mine, dev(dy=n), FK.at[k, x, (y + SIDE - n) % SIDE])

    def weight_6():
        for n in (2, 1, 3):
            take(("vy", n))
        mine = FK.at[k, x]
        for n in (2, 1, 3):
            send(("vx", n), mine, mine, dev(dx=n), FK.at[k, (x + SIDE - n) % SIDE])

    def weight_7():
        for n in (2, 1, 3):
            take(("vx", n))
        send(("vk",), FK.at[k], FK.at[k], dev(dk=1), FK.at[1 - k])

    def weight_8():
        take(("vk",))
        for n in range(SIDE):
            gw_o[:, n * TILE : (n + 1) * TILE] = FK[:, :, :, n, 0:16, :].reshape(512, TILE)
            gb_o[:, n * TILE : (n + 1) * TILE] = jnp.broadcast_to(
                jnp.sum(FK[0, 0, 0, n, 16:24, :], axis=0, keepdims=True), (8, TILE)
            )

    order = [(a, h) for a in ("far", "relay", "near", "mine") for h in range(2)]

    def offset(c, name):
        e = first_way(c)
        return {"far": 2, "relay": e, "near": -e, "mine": 0}[name]

    def group_way(name):
        return 1 if name in ("far", "mine") else -1

    def back_0(c, n):
        name, h = order[n]
        a, e = offset(c, name), group_way(name)
        bs = (2, -e, e, 0)
        lhs = jnp.concatenate(
            [
                jnp.concatenate(
                    [BT[tbl[at_k(h, a, b) * IBLOCKS + i]] for i in range(IBLOCKS)], axis=1
                )
                for b in bs
            ],
            axis=0,
        )
        rhs = DG[c].reshape(2048, WIDE)
        value = jnp.dot(lhs, rhs, preferred_element_type=F32)
        SB[c, n, 0:2] = value[0:256].astype(BF16).reshape(2, TILE, WIDE)
        TK[c, n] = value[256:512].reshape(2, TILE, WIDE)
        send(("bf", c, n), SB.at[c, n, 0], SR.at[c, n, 0], along(h, False, e))
        send(("bd", c, n), SB.at[c, n, 1], SR.at[c, n, 1], along(h, False, -e))

    def back_1(c, n):
        name, h = order[n]
        e = group_way(name)
        take(("bf", c, n))
        SB[c, n, 2] = (TK[c, n, 0] + SR[c, n, 0].astype(F32)).astype(BF16)
        send(("br", c, n), SB.at[c, n, 2], SR.at[c, n, 2], along(h, False, e))

    def back_2(c, n):
        name, h = order[n]
        e = first_way(c)
        take(("bd", c, n))
        value = TK[c, n, 1] + SR[c, n, 1].astype(F32)
        take(("br", c, n))
        value = value + SR[c, n, 2].astype(F32)
        late = 8 + h
        if name == "far":
            SB[c, late, 0] = value.astype(BF16)
            send(("tf", c, h), SB.at[c, late, 0], SR.at[c, late, 0], along(h, True, e))
        elif name == "near":
            SB[c, late, 1] = value.astype(BF16)
            send(("td", c, h), SB.at[c, late, 1], SR.at[c, late, 1], along(h, True, -e))
        elif name == "relay":
            take(("tf", c, h))
            SB[c, late, 2] = (value + SR[c, late, 0].astype(F32)).astype(BF16)
            send(("tr", c, h), SB.at[c, late, 2], SR.at[c, late, 2], along(h, True, e))
        else:
            UK[c, h] = value

    def back_3(c, h):
        late = 8 + h
        take(("td", c, h))
        value = UK[c, h] + SR[c, late, 1].astype(F32)
        take(("tr", c, h))
        value = value + SR[c, late, 2].astype(F32)
        gf_o[h * TILE : (h + 1) * TILE, c * WIDE : (c + 1) * WIDE] = value.astype(BF16)

    spread_0(0)
    spread_0(1)
    weight_0()
    spread_1(0)
    spread_1(1)
    spread_2(0)
    weight_1()
    spread_3(0)

    total = CHUNKS * 8
    extra = {
        1: lambda: spread_2(1),
        4: weight_2,
        7: weight_3,
        9: weight_4,
        11: weight_5,
        13: weight_6,
        17: weight_7,
    }
    for n in range(total + 4):
        if n == 8:
            spread_3(1)
        if n < total:
            back_0(n // 8, n % 8)
        if 0 <= n - 2 < total:
            back_1((n - 2) // 8, (n - 2) % 8)
        if 0 <= n - 4 < total:
            back_2((n - 4) // 8, (n - 4) % 8)
        if n in extra:
            extra[n]()
        if n == 14:
            for h in range(2):
                back_3(0, h)
    weight_8()
    for h in range(2):
        back_3(1, h)

    assert len(messages) == MESSAGES, len(messages)
    for copy, _ in messages.values():
        copy.wait_send()


def pick_table(block_rows, block_cols, block_count):
    ri = lax.axis_index("row")
    ci = lax.axis_index("col")
    y, z = ri // SIDE, ri % SIDE
    x, k = ci // 2, ci % 2
    turn = 1 - 2 * k
    place = jnp.arange(KBLOCKS * IBLOCKS, dtype=jnp.int32)
    kk, ii = place // IBLOCKS, place % IBLOCKS
    from_row = ((y + kk // 8) % SIDE) * SIDE + (z + (kk // 2) % SIDE) % SIDE
    column = from_row * 2 + kk % 2
    dk, dx = ii // 8, (ii // 2) % SIDE
    to_col = ((x + turn * dx + SIDE) % SIDE) * 2 + (k + dk) % 2
    row = to_col * 2 + ii % 2
    wanted = row * KBLOCKS + column
    slot = jnp.arange(SLOTS, dtype=jnp.int32)
    held = jnp.where(slot < block_count, block_rows * KBLOCKS + block_cols, -1)
    match = wanted[:, None] == held[None, :]
    return SLOTS + jnp.sum(jnp.where(match, slot[None, :] - SLOTS, 0), axis=1)


def shards(features, blocks, block_rows, block_cols, block_count, weight, bias_vector, upstream):
    scale = 1.0 / math.sqrt(features.shape[0] * SIDE * SIDE * SIDE * 2)
    table = pick_table(block_rows[0, 0], block_cols[0, 0], block_count[0, 0])
    vmem = pl.BlockSpec(memory_space=pltpu.VMEM)
    hbm = pl.BlockSpec(memory_space=pl.ANY)
    activated, grad_features, grad_weight, grad_bias = pl.pallas_call(
        functools.partial(step_kernel, scale),
        out_shape=(
            jax.ShapeDtypeStruct((256, 512), BF16),
            jax.ShapeDtypeStruct((256, 512), BF16),
            jax.ShapeDtypeStruct((512, 512), F32),
            jax.ShapeDtypeStruct((8, 512), F32),
        ),
        in_specs=[pl.BlockSpec(memory_space=pltpu.SMEM), hbm, hbm, hbm, vmem, hbm],
        out_specs=(vmem, vmem, vmem, vmem),
        scratch_shapes=[
            pltpu.VMEM((CHUNKS, KBLOCKS, TILE, WIDE), BF16),
            pltpu.VMEM((SLOTS + 1, TILE, TILE), BF16),
            pltpu.VMEM((SLOTS + 1, TILE, TILE), BF16),
            pltpu.VMEM((512, 512), BF16),
            pltpu.VMEM((256, 512), BF16),
            pltpu.VMEM((CHUNKS, 4, 512, WIDE), F32),
            pltpu.VMEM((CHUNKS, SIDE, 256, WIDE), BF16),
            pltpu.VMEM((CHUNKS, SIDE, 256, WIDE), BF16),
            pltpu.VMEM((CHUNKS, 3, 256, WIDE), BF16),
            pltpu.VMEM((CHUNKS, 3, 256, WIDE), BF16),
            pltpu.VMEM((256, 512), BF16),
            pltpu.VMEM((256, 512), BF16),
            pltpu.VMEM((CHUNKS, 2 * SIDE, 256, WIDE), BF16),
            pltpu.VMEM((CHUNKS, 8, 2, TILE, WIDE), F32),
            pltpu.VMEM((CHUNKS, 2, TILE, WIDE), F32),
            pltpu.VMEM((CHUNKS, 10, 3, TILE, WIDE), BF16),
            pltpu.VMEM((CHUNKS, 10, 3, TILE, WIDE), BF16),
            pltpu.VMEM((2, SIDE, SIDE, 24, 512), F32),
            pltpu.VMEM((SIDE, SIDE, 24, 512), F32),
            pltpu.VMEM((SIDE, SIDE, 24, 512), F32),
            pltpu.VMEM((3, SIDE, 24, 512), F32),
            pltpu.VMEM((SIDE, 24, 512), F32),
            pltpu.VMEM((3, 24, 512), F32),
            pltpu.VMEM((SIDE, 24, TILE), F32),
            pltpu.VMEM((3, 24, TILE), F32),
            pltpu.VMEM((2, SIDE, SIDE, SIDE, 24, TILE), F32),
            pltpu.SemaphoreType.DMA((7,)),
            pltpu.SemaphoreType.DMA((MESSAGES,)),
            pltpu.SemaphoreType.DMA((MESSAGES,)),
        ],
        compiler_params=pltpu.CompilerParams(
            collective_id=0, has_side_effects=True, vmem_limit_bytes=60 * 2**20
        ),
        name="graph_layer",
    )(table, features, blocks[0, 0], weight, bias_vector.reshape(1, 512), upstream)
    return (activated, grad_weight, grad_bias[0], grad_features)


def solution(mesh):
    in_specs = (
        P(("col", "row"), None),
        P("row", "col", None, None, None),
        P("row", "col", None),
        P("row", "col", None),
        P("row", "col"),
        P(),
        P(),
        P(("row", "col"), None),
    )
    out_specs = (P(("row", "col"), None), P(), P(), P(("col", "row"), None))
    return jax.shard_map(shards, mesh=mesh, in_specs=in_specs, out_specs=out_specs, check_vma=False)
```

time: 433 us -> 120 us (0.28)
  waiting for transfers between devices: 235 us -> 0 us
  Pallas kernels: 0 us -> 110 us
  blocking collectives: 66.8 us -> 0 us
  other arithmetic: 65.6 us -> 1.39 us
  matrix products: 27.3 us -> 0 us
  local copies, waits for them, and re-layouts: 23.9 us -> 5.98 us
  between operations: 13.8 us -> 1.34 us
    reduce_scatter x2 -> x0, waiting for transfers between devices: 124 us -> none  [the longest x1 86.4 us: shards(): lax.psum_scatter(grad_partial, 'row', scatter_dimension=0, tiled=True)]
    pallas_call x0 -> x1, Pallas kernels: none -> 110 us  [shards(): pl.pallas_call(functools.partial(step_kernel, scale), out_shape=(jax.Shap...]
    all_gather x2 -> x0, waiting for transfers between devices: 77.5 us -> none  [the longest x1 56.2 us: shards(): gathered = lax.all_gather(features, 'row', axis=0, tiled=True)]
    psum x1 -> x0, blocking collectives: 66.8 us -> none  [shards(): grad_weight, grad_bias = lax.psum((grad_weight, grad_bias), ('row', 'col'))]
    scatter-add x6 -> x0, other arithmetic: 56.5 us -> none  [one_turn(): return totals.at[put_now].add(product)]
    psum x1 -> x0, waiting for transfers between devices: 32.1 us -> none  [shards(): grad_weight, grad_bias = lax.psum((grad_weight, grad_bias), ('row', 'col'))]
    dot_general x9 -> x0, matrix products: 27.3 us -> none  [the longest x6 22.6 us: one_turn(): jnp.einsum(form, chosen, picked, preferred_element_type=jnp.float32)]
    gather x6 -> x0, local copies, waits for them, and re-layouts: 15.5 us -> none  [one_turn(): picked = source_blocks[take_now]]
  transfers between devices with their start and end apart: 5 -> 0, of which waited for: 5 -> 0; matrix products, arithmetic and copies ran while one was open for 14% -> 0% of each run, Pallas kernels for 0% -> 0%
where the time goes in v1:
time: 120 us; the launch traced here: 119 us
  Pallas kernels  110 us (92%)
  local copies, waits for them, and re-layouts  5.98 us (5%)
  other arithmetic  1.39 us (1%)
  between operations  1.34 us (1%)
    pallas_call x1, Pallas kernels, shards(): pl.pallas_call(functools.partial(step_kernel, scale), out_shape=(jax.Shap...  110 us
    unnamed x5, local copies, waits for them, and re-layouts  4.64 us

profile of v1, /device:TPU:0, one launch (start us, length us, event | category | flops | bytes accessed | tf_op | source)
XLA Modules:
  0.0 119.1 jit_solution(4026969980007735149)
XLA Ops:
  1.4 0.7 compare_select_fusion
  2.0 0.1 select_reduce_fusion
  2.1 0.6 broadcast_add_fusion.tbl
  2.7 110.4 %graph_layer.1 = (bf16[256,512]{1,0:T(8,128)(2,1)}, bf16[256,512]{1,0:T(8,128)(2,1)}, f32[512,512]{1,0:T(8,128)}, f32[8,512]{1,0:T(8,128)}) custom-call(s32[512]{0:T(512)} %broadcast_add_fusion.tbl, bf16[256,512]{1,0:T(8,128)(2,1)} %feat.1, bf16[48,128,128]{2,1,0:T(8,128)(2,1)} %bitcast.7, bf16[512,512]{1,0:T(8,128)(2,1)} %weight.1, f32[1,512]{1,0:T(1,128)} %bitcast.8, ...), custom_call_target="tpu_custom_call" | custom-call | tf_op jit(solution)/shard_map/graph_layer/pallas_call | solution.py:620
  113.1 0.0 copy-start
  113.2 1.3 %slice.3 = f32[1,512]{1,0:T(1,128)} slice(f32[8,512]{1,0:T(8,128)} %get-tuple-element.10), slice={[0:1], [0:512]} | slice | bytes 4096 | tf_op jit(solution)/shard_map/slice | solution.py:666
  114.5 1.7 %copy.16 = bf16[256,512]{1,0:T(8,128)(2,1)} copy(bf16[256,512]{1,0:T(8,128)(2,1)} %get-tuple-element.18) | data formatting | bytes 524288
  116.2 2.3 %copy.17 = f32[512,512]{1,0:T(8,128)} copy(f32[512,512]{1,0:T(8,128)} %get-tuple-element.19) | data formatting | bytes 2097152
  118.4 0.0 copy-done
  118.4 0.7 copy.18
  (1 shorter events, 0.0 us)
Async XLA Ops:
  113.1 5.3 %copy-start = (bf16[256,512]{1,0:T(8,128)(2,1)S(1)}, bf16[256,512]{1,0:T(8,128)(2,1)}, u32[]{:S(2)}) copy-start(bf16[256,512]{1,0:T(8,128)(2,1)} %get-tuple-element.21) | copy-start | bytes 786436

commit v2 on v0

v2 whole, which is shorter than its diff:
```python
import functools
import math

import jax
import jax.numpy as jnp
from jax import lax
from jax.experimental import pallas as pl
from jax.experimental.pallas import tpu as pltpu
from jax.sharding import PartitionSpec as P

MESH = pl.DeviceIdType.MESH
F32 = jnp.float32
BF16 = jnp.bfloat16
SIDE = 4
TILE = 128
WIDE = 256
CHUNKS = 2
KBLOCKS = 32
IBLOCKS = 16
SLOTS = 48
SLOTS_AT_ONCE = 16
FAR = 1 << 17
GROUPS = 88


def wrap(value):
    return value % SIDE


def at_k(h, a, b):
    a, b = wrap(a), wrap(b)
    dy, dz = (a, b) if h == 0 else (b, a)
    return (dy * SIDE + dz) * 2 + h


def step_kernel(
    scale,
    count,
    rows_in,
    cols_in,
    feat,
    blocks,
    weight,
    bias,
    ups,
    act_o,
    gf_o,
    gw_o,
    gb_o,
    G0,
    G1,
    BK,
    BT,
    WT,
    UP,
    Z0,
    Z1,
    S1,
    R0,
    XS,
    XR,
    HD,
    DP,
    DG0,
    DG1,
    UK,
    SB,
    SR,
    GP,
    AK,
    PX,
    PR,
    XA,
    XB,
    FK,
    LIKE,
    AO,
    FO,
    WO,
    BO,
    IX,
    TV,
    TS,
    lsem,
    ssem,
    rsem,
):
    G, Z, DG = (G0, G1), (Z0, Z1), (DG0, DG1)
    ri = lax.axis_index("row")
    ci = lax.axis_index("col")
    y, z = ri // SIDE, ri % SIDE
    x, k = ci // 2, ci % 2
    turn = 1 - 2 * k

    def dev(dy=0, dz=0, dx=0, dk=0):
        row = ((y + dy + SIDE) % SIDE) * SIDE + (z + dz + SIDE) % SIDE
        col = ((x + dx + SIDE) % SIDE) * 2 + (k + dk) % 2
        return (row, col)

    def along(h, first, step):
        if (h == 0) == first:
            return dev(dy=step)
        return dev(dz=step)

    groups = {}

    def send(group, src, dst, to, out=None):
        number = groups.setdefault(group, len(groups))
        pltpu.make_async_remote_copy(
            src_ref=src,
            dst_ref=dst,
            send_sem=ssem.at[group[1] if out is None else out],
            recv_sem=rsem.at[number],
            device_id=to,
            device_id_type=MESH,
        ).start()

    def wait_bytes(like, sem):
        pltpu.make_async_copy(like, like, sem).wait()

    def take(group, units):
        wait_bytes(G[group[1]].at[pl.ds(0, units)], rsem.at[groups[group]])

    local = []

    def fetch(src, dst):
        copy = pltpu.make_async_copy(src, dst, lsem.at[len(local)])
        copy.start()
        local.append(copy)
        return copy

    own = [
        [
            fetch(
                feat.at[pl.ds(h * TILE, TILE), pl.ds(c * WIDE, WIDE)],
                G[c].at[at_k(h, 0, 0)],
            )
            for h in range(2)
        ]
        for c in range(CHUNKS)
    ]
    blocks_in = fetch(blocks, BK)
    weight_in = fetch(weight, WT)
    ups_in = fetch(ups, UP)

    barrier = pltpu.get_barrier_semaphore()
    partners = [dev(dk=1)]
    for step in (1, -1):
        partners += [dev(dy=step), dev(dz=step), dev(dx=step)]
    for partner in partners:
        pl.semaphore_signal(barrier, inc=1, device_id=partner, device_id_type=MESH)
    for c in range(CHUNKS):
        Z[c][SLOTS] = jnp.zeros((TILE, WIDE), F32)
    IX[...] = jnp.zeros_like(IX)
    IX[0:1, 0:SLOTS] = rows_in[...]
    IX[8:9, 0:SLOTS] = cols_in[...]
    pl.semaphore_wait(barrier, len(partners))

    def first_way(c):
        return 1 if c == 0 else -1

    def second_way(a):
        return 1 if a in (0, 1) else -1

    def second_sends(c, a):
        for h in range(2):
            src = G[c].at[at_k(h, a, 0)]
            for step in (1, -1):
                side = "in" if step == second_way(a) else "by"
                name = "all" if side == "by" and a in (1, -1) else a
                send(
                    ("g2" + side, c, name),
                    src,
                    G[c].at[at_k(h, a, -step)],
                    along(h, False, step),
                )

    def gather_0(c):
        for h in range(2):
            own[c][h].wait()
            src = G[c].at[at_k(h, 0, 0)]
            for step in (first_way(c), -first_way(c)):
                side = "in" if step == first_way(c) else "by"
                send(("g1" + side, c), src, G[c].at[at_k(h, -step, 0)], along(h, True, step))

    def gather_own(c):
        second_sends(c, 0)

    def gather_1(c):
        e = first_way(c)
        take(("g1in", c), 2)
        for h in range(2):
            send(
                ("g1r", c),
                G[c].at[at_k(h, -e, 0)],
                G[c].at[at_k(h, 2, 0)],
                along(h, True, e),
            )
        second_sends(c, -e)
        take(("g1by", c), 2)
        second_sends(c, e)

    def second_relay(c, a):
        e = second_way(a)
        take(("g2in", c, a), 2)
        for h in range(2):
            send(
                ("g2r", c, "all" if a in (1, -1) else a),
                G[c].at[at_k(h, a, -e)],
                G[c].at[at_k(h, a, 2)],
                along(h, False, e),
            )

    def gather_2(c):
        second_relay(c, 0)

    def gather_3(c):
        take(("g1r", c), 2)
        second_sends(c, 2)

    def gather_4(c):
        second_relay(c, first_way(c) * -1)
        second_relay(c, first_way(c))

    def gather_6(c):
        second_relay(c, 2)

    def gather_8(c):
        take(("g2by", c, 0), 2)
        take(("g2by", c, "all"), 4)
        take(("g2by", c, 2), 2)
        take(("g2r", c, 0), 2)
        take(("g2r", c, "all"), 4)
        take(("g2r", c, 2), 2)

    def tables_0():
        lane = lax.broadcasted_iota(jnp.int32, (TILE, TILE), 1)
        down = lax.broadcasted_iota(jnp.int32, (TILE, TILE), 0)
        rows = jnp.broadcast_to(IX[0:1, :], (TILE, TILE))
        cols = jnp.broadcast_to(IX[8:9, :], (TILE, TILE))
        live = lane < count[0, 0]
        for which, key in enumerate((rows * KBLOCKS + cols, cols * IBLOCKS + rows)):
            shift = 5 if which == 0 else 4
            key = jnp.where(live, key, FAR + lane)
            key_down = key.T
            own, other = key_down >> shift, key_down & ((1 << shift) - 1)
            less = key < key_down
            rank = jnp.sum(jnp.where(less, 1, 0), axis=1, keepdims=True)
            same = less & ((key >> shift) == own)
            keep = jnp.minimum(jnp.sum(jnp.where(same, 1, 0), axis=1, keepdims=True), 1)
            if which == 0:
                piece = other >> 1
                dy = ((piece >> 2) + SIDE - y) & 3
                dz = (piece + SIDE - z) & 3
                place = (dy * SIDE + dz) * 2 + (other & 1)
            else:
                to_col = other >> 1
                dx = (turn * ((to_col >> 1) - x)) & 3
                dk = (to_col + 2 - k) & 1
                place = (dk * SIDE + dx) * 2 + (other & 1)
            hit = rank == lane
            upto = jnp.sum(jnp.where(own <= lane, 1, 0), axis=0, keepdims=True)
            any_own = jnp.sum(jnp.where(own == lane, 1, 0), axis=0, keepdims=True)
            at = which * 8
            TV[at : at + 1, :] = jnp.sum(jnp.where(hit, down, 0), axis=0, keepdims=True)
            TV[at + 1 : at + 2, :] = jnp.sum(jnp.where(hit, place, 0), axis=0, keepdims=True)
            TV[at + 2 : at + 3, :] = jnp.sum(jnp.where(hit, keep, 0), axis=0, keepdims=True)
            TV[at + 3 : at + 4, :] = jnp.where(any_own > 0, upto - 1, SLOTS)

    def tables_1():
        copy = pltpu.make_async_copy(TV, TS, lsem.at[7])
        copy.start()
        copy.wait()

    def product(c, which, part):
        at = which * 8
        base = part * SLOTS_AT_ONCE
        total = None if part == 0 else Z[c][base - 1]
        for slot in range(base, base + SLOTS_AT_ONCE):
            place = TS[at + 1, slot]
            block = (BK if which == 0 else BT)[TS[at, slot]]
            value = jnp.dot(block, (G if which == 0 else DG)[c][place], preferred_element_type=F32)
            if total is not None:
                value = value + total * TS[at + 2, slot].astype(F32)
            Z[c][slot] = value
            total = value

    def multiply(c, part):
        product(c, 0, part)

    def multiply_back(c, part):
        product(c, 1, part)

    def part_of(c, dk, dx):
        row = (((x + turn * dx + SIDE) % SIDE) * 2 + (k + dk) % 2) * 2
        return jnp.concatenate([Z[c][TS[3, row]], Z[c][TS[3, row + 1]]], axis=0)

    def reduce_0(c):
        for dx in (2, 3, 1, 0):
            S1[c, dx] = part_of(c, 1, dx).astype(BF16)
            mirrored = wrap(-dx)
            send(("c0", c, mirrored), S1.at[c, dx], R0.at[c, mirrored], dev(dk=1))

    def paired(c, dx):
        take(("c0", c, dx), 2)
        return part_of(c, 0, dx) + R0[c, dx].astype(F32)

    def reduce_1(c):
        XS[c, 0] = paired(c, 2).astype(BF16)
        for half in range(2):
            lines = pl.ds(half * TILE, TILE)
            send(("cf", c, half), XS.at[c, 0, lines], XR.at[c, 0, lines], dev(dx=turn))
        XS[c, 1] = paired(c, 3).astype(BF16)
        send(("cd", c), XS.at[c, 1], XR.at[c, 1], dev(dx=-turn))

    def reduce_2(c):
        value = paired(c, 1)
        for half in range(2):
            lines = pl.ds(half * TILE, TILE)
            part = value[half * TILE : (half + 1) * TILE]
            take(("cf", c, half), 1)
            XS[c, 2, lines] = (part + XR[c, 0, lines].astype(F32)).astype(BF16)
            send(("cr", c), XS.at[c, 2, lines], XR.at[c, 2, lines], dev(dx=turn))

    def reduce_3(c):
        value = paired(c, 0)
        take(("cd", c), 2)
        value = value + XR[c, 1].astype(F32)
        take(("cr", c), 2)
        value = value + XR[c, 2].astype(F32)
        HD[:, c * WIDE : (c + 1) * WIDE] = value.astype(BF16)

    def turn_blocks(part):
        @pl.loop(0, SLOTS_AT_ONCE // 4)
        def _(n):
            for j in range(4):
                s = part * SLOTS_AT_ONCE + n * 4 + j
                BT[s] = BK[s].T

    gather_0(0)
    gather_own(0)
    gather_0(1)
    tables_0()
    blocks_in.wait()
    turn_blocks(0)
    tables_1()
    gather_1(0)
    gather_own(1)
    gather_2(0)
    turn_blocks(1)
    gather_1(1)
    gather_3(0)
    gather_4(0)
    turn_blocks(2)
    gather_2(1)
    gather_6(0)
    gather_3(1)
    gather_8(0)
    multiply(0, 0)
    gather_4(1)
    multiply(0, 1)
    multiply(0, 2)
    reduce_0(0)
    gather_6(1)
    reduce_1(0)
    reduce_2(0)
    gather_8(1)
    multiply(1, 0)
    multiply(1, 1)
    multiply(1, 2)
    reduce_0(1)
    reduce_3(0)
    reduce_1(1)
    reduce_2(1)
    weight_in.wait()
    ups_in.wait()
    reduce_3(1)

    bias_rows = []
    for n in range(CHUNKS):
        columns = slice(n * WIDE, (n + 1) * WIDE)
        pre = jnp.dot(HD[...], WT[:, columns], preferred_element_type=F32) + bias[:, columns]
        sig = jax.nn.sigmoid(pre)
        AO[:, columns] = (pre * sig).astype(BF16)
        dpre = (UP[:, columns].astype(F32) * sig * (1.0 + pre * (1.0 - sig))).astype(BF16)
        DP[:, columns] = dpre
        bias_rows.append(jnp.sum(dpre.astype(F32).reshape(32, 8, WIDE), axis=0))

    def hidden(c, place):
        return DG[c].at[pl.ds(2 * place, 2)]

    def spread_0(c):
        value = lax.dot_general(
            DP[...],
            WT[pl.ds(c * WIDE, WIDE), :],
            (((1,), (1,)), ((), ())),
            preferred_element_type=F32,
        )
        DG[c][0:2] = value.astype(BF16).reshape(2, TILE, WIDE)
        for half in range(2):
            send(("sp", c, half), DG[c].at[half], DG[c].at[6 + half], dev(dx=turn))
        send(("sm", c), hidden(c, 0), hidden(c, 1), dev(dx=-turn))
        send(("sc", c), hidden(c, 0), hidden(c, SIDE), dev(dk=1))

    def spread_1(c):
        for half in range(2):
            take(("sp", c, half), 1)
            send(("sr", c), DG[c].at[6 + half], DG[c].at[4 + half], dev(dx=turn))
        send(("sc", c), hidden(c, 3), hidden(c, SIDE + 1), dev(dk=1))
        take(("sm", c), 2)
        send(("sc", c), hidden(c, 1), hidden(c, SIDE + 3), dev(dk=1))

    def spread_2(c):
        take(("sr", c), 2)
        send(("sc", c), hidden(c, 2), hidden(c, SIDE + 2), dev(dk=1))

    def spread_3(c):
        take(("sc", c), 8)

    plane = [(dy, dz) for dy in range(SIDE) for dz in range(SIDE) if dy or dz]

    def weight_0():
        value = lax.dot_general(
            HD[...], DP[...], (((0,), (0,)), ((), ())), preferred_element_type=F32
        )
        for zz in range(SIDE):
            lanes = slice(zz * TILE, (zz + 1) * TILE)
            tiles = value[:, lanes].reshape(2, SIDE, SIDE, 16, TILE)
            sums = bias_rows[zz // 2][:, (zz % 2) * TILE : (zz % 2 + 1) * TILE]
            for yy in range(SIDE):
                GP[:, yy * SIDE + zz, :, 0:16, :] = tiles[:, :, yy]
                GP[:, yy * SIDE + zz, :, 16:24, :] = jnp.broadcast_to(
                    sums, (2, SIDE, 8, TILE)
                )
        send(("wk",), GP.at[1 - k], AK, dev(dk=1), out=2)

    def weight_1():
        wait_bytes(AK, rsem.at[groups[("wk",)]])
        AK[...] = GP[k] + AK[...]
        PX[...] = AK[...].astype(BF16)
        for n, (dy, dz) in enumerate(plane):
            there = ((y + dy) % SIDE) * SIDE + (z + dz) % SIDE
            send(("wp",), PX.at[there], PR.at[n], dev(dy=dy, dz=dz), out=3)

    def weight_2():
        wait_bytes(PR, rsem.at[groups[("wp",)]])
        value = AK[ri]
        for n in range(len(plane)):
            value = value + PR[n].astype(F32)
        XA[...] = value
        for n in (2, 1, 3):
            send(("wx",), XA.at[(x + n) % SIDE], XB.at[n - 1], dev(dx=n), out=4)

    def weight_3():
        wait_bytes(XB, rsem.at[groups[("wx",)]])
        value = XA[x]
        for n in range(3):
            value = value + XB[n]
        FK[k, x, ri] = (value * scale).astype(BF16)
        mine = FK.at[k, x, ri]
        for dy, dz in plane:
            send(("vp",), mine, mine, dev(dy=dy, dz=dz), out=5)

    def weight_4():
        wait_bytes(LIKE, rsem.at[groups[("vp",)]])
        mine = FK.at[k, x]
        for n in (2, 1, 3):
            send(("vx",), mine, mine, dev(dx=n), out=6)

    def weight_5():
        wait_bytes(FK.at[0, pl.ds(0, 3)], rsem.at[groups[("vx",)]])
        send(("vk",), FK.at[k], FK.at[k], dev(dk=1), out=7)

    def weight_6():
        wait_bytes(FK.at[0], rsem.at[groups[("vk",)]])
        for yy in range(SIDE):
            for zz in range(SIDE):
                lanes = slice(zz * TILE, (zz + 1) * TILE)
                for kk in range(2):
                    for xx in range(SIDE):
                        first = kk * 256 + xx * 64 + yy * 16
                        WO[first : first + 16, lanes] = FK[kk, xx, yy * SIDE + zz, 0:16, :].astype(F32)
        for zz in range(SIDE):
            BO[:, zz * TILE : (zz + 1) * TILE] = jnp.sum(
                FK[0, 0, zz, 16:24, :].astype(F32), axis=0, keepdims=True
            )

    def offset(c, name):
        e = first_way(c)
        return {"far": 2, "relay": e, "near": -e, "mine": 0}[name]

    def group_way(name):
        return 1 if name in ("far", "mine") else -1

    def sum_of(c, h, a, b):
        dy, dz = (a, b) if h == 0 else (b, a)
        column = (((y + dy + SIDE) % SIDE) * SIDE + (z + dz + SIDE) % SIDE) * 2 + h
        return Z[c][TS[8 + 3, column]]

    NAMES = ("far", "relay", "near", "mine")

    def back_0(c, i):
        name = NAMES[i]
        a, e = offset(c, name), group_way(name)
        for h in range(2):
            SB[c, h, i, 0] = sum_of(c, h, a, 2).astype(BF16)
            send(("bf", c, i), SB.at[c, h, i, 0], SR.at[c, h, i, 0], along(h, False, e))
        for h in range(2):
            SB[c, h, i, 1] = sum_of(c, h, a, -e).astype(BF16)
            send(("bd", c, i), SB.at[c, h, i, 1], SR.at[c, h, i, 1], along(h, False, -e))

    def back_1(c, i):
        name = NAMES[i]
        a, e = offset(c, name), group_way(name)
        take(("bf", c, i), 2)
        for h in range(2):
            SB[c, h, i, 2] = (sum_of(c, h, a, e) + SR[c, h, i, 0].astype(F32)).astype(BF16)
            send(("br", c, i), SB.at[c, h, i, 2], SR.at[c, h, i, 2], along(h, False, e))

    def back_2(c, i):
        name = NAMES[i]
        e = first_way(c)
        take(("bd", c, i), 2)
        take(("br", c, i), 2)
        if name == "relay":
            take(("tf", c), 2)
        for h in range(2):
            value = sum_of(c, h, offset(c, name), 0) + SR[c, h, i, 1].astype(F32)
            value = value + SR[c, h, i, 2].astype(F32)
            if name == "far":
                SB[c, h, 4, 0] = value.astype(BF16)
                send(("tf", c), SB.at[c, h, 4, 0], SR.at[c, h, 4, 0], along(h, True, e))
            elif name == "near":
                SB[c, h, 4, 1] = value.astype(BF16)
                send(("td", c), SB.at[c, h, 4, 1], SR.at[c, h, 4, 1], along(h, True, -e))
            elif name == "relay":
                SB[c, h, 4, 2] = (value + SR[c, h, 4, 0].astype(F32)).astype(BF16)
                send(("tr", c), SB.at[c, h, 4, 2], SR.at[c, h, 4, 2], along(h, True, e))
            else:
                UK[c, h] = value

    def back_3(c):
        take(("td", c), 2)
        take(("tr", c), 2)
        for h in range(2):
            value = UK[c, h] + SR[c, h, 4, 1].astype(F32)
            value = value + SR[c, h, 4, 2].astype(F32)
            FO[h * TILE : (h + 1) * TILE, c * WIDE : (c + 1) * WIDE] = value.astype(BF16)

    out = []

    def leave(src, dst):
        copy = pltpu.make_async_copy(src, dst, lsem.at[8 + len(out)])
        copy.start()
        out.append(copy)

    spread_0(0)
    weight_0()
    leave(AO, act_o)
    spread_1(0)
    spread_0(1)
    weight_1()
    spread_2(0)
    spread_3(0)
    for part in range(3):
        multiply_back(0, part)
    for i in range(4):
        back_0(0, i)
    spread_1(1)
    weight_2()
    spread_2(1)
    back_1(0, 0)
    back_1(0, 1)
    spread_3(1)
    for part in range(3):
        multiply_back(1, part)
    back_0(1, 0)
    back_1(0, 2)
    back_0(1, 1)
    back_2(0, 0)
    back_1(0, 3)
    back_0(1, 2)
    back_2(0, 1)
    back_0(1, 3)
    weight_3()
    back_1(1, 0)
    back_2(0, 2)
    back_2(0, 3)
    back_1(1, 1)
    back_1(1, 2)
    back_3(0)
    leave(FO.at[:, pl.ds(0, WIDE)], gf_o.at[:, pl.ds(0, WIDE)])
    back_2(1, 0)
    back_1(1, 3)
    weight_4()
    back_2(1, 1)
    back_2(1, 2)
    back_2(1, 3)
    weight_5()
    weight_6()
    leave(WO, gw_o)
    leave(BO, gb_o)
    back_3(1)
    leave(FO.at[:, pl.ds(WIDE, WIDE)], gf_o.at[:, pl.ds(WIDE, WIDE)])
    for copy in out:
        copy.wait()

    assert len(groups) == GROUPS, len(groups)
    for c in range(CHUNKS):
        wait_bytes(Z[c].at[pl.ds(0, 44)], ssem.at[c])
    for number, like in enumerate(
        (AK, PR, XB, LIKE, FK.at[0, pl.ds(0, 3)], FK.at[0]), start=CHUNKS
    ):
        wait_bytes(like, ssem.at[number])


def finish_kernel(a, b, c, d, ao, bo, co, do, av, bv, cv, dv, sem):
    pairs = ((c, cv, co), (a, av, ao), (b, bv, bo), (d, dv, do))
    copies_in = [pltpu.make_async_copy(p[0], p[1], sem.at[n]) for n, p in enumerate(pairs)]
    copies_out = [pltpu.make_async_copy(p[1], p[2], sem.at[4 + n]) for n, p in enumerate(pairs)]
    for copy in copies_in:
        copy.start()
    for copy_in, copy_out in zip(copies_in, copies_out):
        copy_in.wait()
        copy_out.start()
    for copy in copies_out:
        copy.wait()


def shards(features, blocks, block_rows, block_cols, block_count, weight, bias_vector, upstream):
    scale = 1.0 / math.sqrt(features.shape[0] * SIDE * SIDE * SIDE * 2)
    vmem = pl.BlockSpec(memory_space=pltpu.VMEM)
    hbm = pl.BlockSpec(memory_space=pl.ANY)
    smem = pl.BlockSpec(memory_space=pltpu.SMEM)
    shapes = (
        jax.ShapeDtypeStruct((256, 512), BF16),
        jax.ShapeDtypeStruct((256, 512), BF16),
        jax.ShapeDtypeStruct((512, 512), F32),
        jax.ShapeDtypeStruct((1, 512), F32),
    )
    results = pl.pallas_call(
        functools.partial(step_kernel, scale),
        out_shape=shapes,
        in_specs=[smem, vmem, vmem, hbm, hbm, hbm, vmem, hbm],
        out_specs=(hbm, hbm, hbm, hbm),
        scratch_shapes=[
            pltpu.VMEM((KBLOCKS, TILE, WIDE), BF16),
            pltpu.VMEM((KBLOCKS, TILE, WIDE), BF16),
            pltpu.VMEM((SLOTS, TILE, TILE), BF16),
            pltpu.VMEM((SLOTS, TILE, TILE), BF16),
            pltpu.VMEM((512, 512), BF16),
            pltpu.VMEM((256, 512), BF16),
            pltpu.VMEM((SLOTS + 1, TILE, WIDE), F32),
            pltpu.VMEM((SLOTS + 1, TILE, WIDE), F32),
            pltpu.VMEM((CHUNKS, SIDE, 256, WIDE), BF16),
            pltpu.VMEM((CHUNKS, SIDE, 256, WIDE), BF16),
            pltpu.VMEM((CHUNKS, 3, 256, WIDE), BF16),
            pltpu.VMEM((CHUNKS, 3, 256, WIDE), BF16),
            pltpu.VMEM((256, 512), BF16),
            pltpu.VMEM((256, 512), BF16),
            pltpu.VMEM((IBLOCKS, TILE, WIDE), BF16),
            pltpu.VMEM((IBLOCKS, TILE, WIDE), BF16),
            pltpu.VMEM((CHUNKS, 2, TILE, WIDE), F32),
            pltpu.VMEM((CHUNKS, 2, 5, 3, TILE, WIDE), BF16),
            pltpu.VMEM((CHUNKS, 2, 5, 3, TILE, WIDE), BF16),
            pltpu.VMEM((2, 16, SIDE, 24, TILE), F32),
            pltpu.VMEM((16, SIDE, 24, TILE), F32),
            pltpu.VMEM((16, SIDE, 24, TILE), BF16),
            pltpu.VMEM((15, SIDE, 24, TILE), BF16),
            pltpu.VMEM((SIDE, 24, TILE), F32),
            pltpu.VMEM((3, 24, TILE), F32),
            pltpu.VMEM((2, SIDE, 16, 24, TILE), BF16),
            pltpu.VMEM((15, 24, TILE), BF16),
            pltpu.VMEM((256, 512), BF16),
            pltpu.VMEM((256, 512), BF16),
            pltpu.VMEM((512, 512), F32),
            pltpu.VMEM((1, 512), F32),
            pltpu.VMEM((16, TILE), jnp.int32),
            pltpu.VMEM((16, TILE), jnp.int32),
            pltpu.SMEM((16, TILE), jnp.int32),
            pltpu.SemaphoreType.DMA((13,)),
            pltpu.SemaphoreType.DMA((CHUNKS + 6,)),
            pltpu.SemaphoreType.DMA((GROUPS,)),
        ],
        compiler_params=pltpu.CompilerParams(
            collective_id=0, has_side_effects=True, vmem_limit_bytes=60 * 2**20
        ),
        name="graph_layer",
    )(
        block_count,
        block_rows[0],
        block_cols[0],
        features,
        blocks[0, 0],
        weight,
        bias_vector.reshape(1, 512),
        upstream,
    )
    activated, grad_features, grad_weight, grad_bias = pl.pallas_call(
        finish_kernel,
        out_shape=shapes,
        in_specs=[hbm] * 4,
        out_specs=(hbm,) * 4,
        scratch_shapes=[pltpu.VMEM(s.shape, s.dtype) for s in shapes]
        + [pltpu.SemaphoreType.DMA((8,))],
        compiler_params=pltpu.CompilerParams(vmem_limit_bytes=60 * 2**20),
        name="finish",
    )(*results)
    return (activated, grad_weight, grad_bias.reshape(512), grad_features)


def solution(mesh):
    in_specs = (
        P(("col", "row"), None),
        P("row", "col", None, None, None),
        P("row", "col", None),
        P("row", "col", None),
        P("row", "col"),
        P(),
        P(),
        P(("row", "col"), None),
    )
    out_specs = (P(("row", "col"), None), P(), P(), P(("col", "row"), None))
    return jax.shard_map(shards, mesh=mesh, in_specs=in_specs, out_specs=out_specs, check_vma=False)
```

time: 433 us -> 94.2 us (0.22)
  waiting for transfers between devices: 235 us -> 0 us
  Pallas kernels: 0 us -> 91.5 us
  blocking collectives: 66.8 us -> 0 us
  other arithmetic: 65.6 us -> 0 us
  matrix products: 27.3 us -> 0 us
  local copies, waits for them, and re-layouts: 23.9 us -> 0 us
  between operations: 13.8 us -> 1.29 us
    reduce_scatter x2 -> x0, waiting for transfers between devices: 124 us -> none  [the longest x1 86.4 us: shards(): lax.psum_scatter(grad_partial, 'row', scatter_dimension=0, tiled=True)]
    pallas_call x0 -> x2, Pallas kernels: none -> 91.5 us  [the longest x1 89.1 us: shards(): pl.pallas_call(functools.partial(step_kernel, scale), out_shape=shapes, i...]
    all_gather x2 -> x0, waiting for transfers between devices: 77.5 us -> none  [the longest x1 56.2 us: shards(): gathered = lax.all_gather(features, 'row', axis=0, tiled=True)]
    psum x1 -> x0, blocking collectives: 66.8 us -> none  [shards(): grad_weight, grad_bias = lax.psum((grad_weight, grad_bias), ('row', 'col'))]
    scatter-add x6 -> x0, other arithmetic: 56.5 us -> none  [one_turn(): return totals.at[put_now].add(product)]
    psum x1 -> x0, waiting for transfers between devices: 32.1 us -> none  [shards(): grad_weight, grad_bias = lax.psum((grad_weight, grad_bias), ('row', 'col'))]
    dot_general x9 -> x0, matrix products: 27.3 us -> none  [the longest x6 22.6 us: one_turn(): jnp.einsum(form, chosen, picked, preferred_element_type=jnp.float32)]
    gather x6 -> x0, local copies, waits for them, and re-layouts: 15.5 us -> none  [one_turn(): picked = source_blocks[take_now]]
  transfers between devices with their start and end apart: 5 -> 0, of which waited for: 5 -> 0; matrix products, arithmetic and copies ran while one was open for 14% -> 0% of each run, Pallas kernels for 0% -> 0%
where the time goes in v2:
time: 94.2 us; the launch traced here: 92.8 us
  Pallas kernels  91.5 us (97%)
  between operations  1.29 us (1%)
    pallas_call x1, Pallas kernels, shards(): pl.pallas_call(functools.partial(step_kernel, scale), out_shape=shapes, i...  89.1 us
    pallas_call x1, Pallas kernels, shards(): pl.pallas_call(finish_kernel, out_shape=shapes, in_specs=[hbm] * 4, out_s...  2.43 us

profile of v2, /device:TPU:0, one launch (start us, length us, event | category | flops | bytes accessed | tf_op | source)
XLA Modules:
  0.0 92.8 jit_solution(11720416200149143462)
XLA Ops:
  1.3 89.1 %graph_layer.1 = (bf16[256,512]{1,0:T(8,128)(2,1)}, bf16[256,512]{1,0:T(8,128)(2,1)}, f32[512,512]{1,0:T(8,128)}, f32[1,512]{1,0:T(1,128)}) custom-call(s32[1,1]{1,0:T(1,128)S(6)} %copy.12.count, s32[1,48]{1,0:T(1,128)} %bitcast.7, s32[1,48]{1,0:T(1,128)} %bitcast.8, bf16[256,512]{1,0:T(8,128)(2,1)} %feat.1, bf16[48,128,128]{2,1,0:T(8,128)(2,1)} %bitcast.5, ...), custom_call_target="tpu_custom_call" | custom-call | tf_op jit(solution)/shard_map/graph_layer/pallas_call | solution.py:641
  90.4 2.4 %finish.1 = (bf16[256,512]{1,0:T(8,128)(2,1)}, bf16[256,512]{1,0:T(8,128)(2,1)}, f32[512,512]{1,0:T(8,128)}, f32[1,512]{1,0:T(1,128)}) custom-call(bf16[256,512]{1,0:T(8,128)(2,1)} %get-tuple-element.12.a, bf16[256,512]{1,0:T(8,128)(2,1)} %get-tuple-element.13.b, f32[512,512]{1,0:T(8,128)} %get-tuple-element.14.c, f32[1,512]{1,0:T(1,128)} %get-tuple-element.15.d), custom_call_target="tpu_custom_call" | custom-call | tf_op jit(solution)/shard_map/finish/pallas_call | solution.py:699

commit v3 on v2

--- a/solution.py
+++ b/solution.py
@@ -15,12 +15,84 @@
 TILE = 128
 WIDE = 256
 CHUNKS = 2
+HALF = 256
 KBLOCKS = 32
 IBLOCKS = 16
 SLOTS = 48
 SLOTS_AT_ONCE = 16
+LOCAL = 2 * CHUNKS + 6
+FORWARD = (
+    ("g0", 0),
+    ("own", 0),
+    ("g0", 1),
+    ("prep",),
+    ("g1", 0),
+    ("own", 1),
+    ("g2", 0),
+    ("turn", 1),
+    ("g1", 1),
+    ("g3", 0),
+    ("g4", 0),
+    ("g2", 1),
+    ("g3", 1),
+    ("turn", 2),
+    ("g6", 0),
+    ("g4", 1),
+    ("g6", 1),
+    ("mm", 0),
+    ("r1", 0),
+    ("mm", 1),
+    ("r2", 0),
+    ("r1", 1),
+    ("r3", 0),
+    ("r2", 1),
+    ("r3", 1),
+)
+BACKWARD = (
+    ("s0", 0),
+    ("w0",),
+    ("s1", 0),
+    ("s0", 1),
+    ("w1",),
+    ("s2", 0),
+    ("mm", 0),
+    ("b0", 0, 0),
+    ("b0", 0, 1),
+    ("b0", 0, 2),
+    ("b0", 0, 3),
+    ("s1", 1),
+    ("w2",),
+    ("s2", 1),
+    ("b1", 0, 0),
+    ("b1", 0, 1),
+    ("mm", 1),
+    ("b0", 1, 0),
+    ("b1", 0, 2),
+    ("b0", 1, 1),
+    ("b1", 0, 3),
+    ("w3",),
+    ("b2", 0, 0),
+    ("b0", 1, 2),
+    ("b0", 1, 3),
+    ("b1", 1, 0),
+    ("b2", 0, 2),
+    ("b1", 1, 1),
+    ("b2", 0, 1),
+    ("b1", 1, 2),
+    ("w4",),
+    ("b2", 1, 0),
+    ("b1", 1, 3),
+    ("b2", 0, 3),
+    ("b2", 1, 2),
+    ("b2", 1, 1),
+    ("b3", 0),
+    ("w5",),
+    ("b2", 1, 3),
+    ("w6",),
+    ("b3", 1),
+)
 FAR = 1 << 17
-GROUPS = 88
+GROUPS = 41 * CHUNKS + 6
 
 
 def wrap(value):
@@ -33,59 +105,13 @@
     return (dy * SIDE + dz) * 2 + h
 
 
-def step_kernel(
-    scale,
-    count,
-    rows_in,
-    cols_in,
-    feat,
-    blocks,
-    weight,
-    bias,
-    ups,
-    act_o,
-    gf_o,
-    gw_o,
-    gb_o,
-    G0,
-    G1,
-    BK,
-    BT,
-    WT,
-    UP,
-    Z0,
-    Z1,
-    S1,
-    R0,
-    XS,
-    XR,
-    HD,
-    DP,
-    DG0,
-    DG1,
-    UK,
-    SB,
-    SR,
-    GP,
-    AK,
-    PX,
-    PR,
-    XA,
-    XB,
-    FK,
-    LIKE,
-    AO,
-    FO,
-    WO,
-    BO,
-    IX,
-    TV,
-    TS,
-    lsem,
-    ssem,
-    rsem,
-):
-    G, Z, DG = (G0, G1), (Z0, Z1), (DG0, DG1)
+def step_kernel(scale, count, rows_in, cols_in, feat, blocks, weight, bias, ups, *refs):
+    AO, FO, WO, BO = refs[:4]
+    refs = refs[4:]
+    G, Z, DG = refs[:CHUNKS], refs[CHUNKS : 2 * CHUNKS], refs[2 * CHUNKS : 3 * CHUNKS]
+    BK, BT, WT, UP, S1, R0, XS, XR, HD, DP, UK, SB, SR = refs[3 * CHUNKS : 3 * CHUNKS + 13]
+    GP, AK, PX, PR, XA, XB, FK, LIKE = refs[3 * CHUNKS + 13 : 3 * CHUNKS + 21]
+    RV, CV, BV, IX, TV, TS, lsem, ssem, rsem = refs[3 * CHUNKS + 21 :]
     ri = lax.axis_index("row")
     ci = lax.axis_index("col")
     y, z = ri // SIDE, ri % SIDE
@@ -141,7 +167,10 @@
     ]
     blocks_in = fetch(blocks, BK)
     weight_in = fetch(weight, WT)
+    rows_got = fetch(rows_in, RV)
+    cols_got = fetch(cols_in, CV)
     ups_in = fetch(ups, UP)
+    bias_in = fetch(bias, BV)
 
     barrier = pltpu.get_barrier_semaphore()
     partners = [dev(dk=1)]
@@ -152,12 +181,10 @@
     for c in range(CHUNKS):
         Z[c][SLOTS] = jnp.zeros((TILE, WIDE), F32)
     IX[...] = jnp.zeros_like(IX)
-    IX[0:1, 0:SLOTS] = rows_in[...]
-    IX[8:9, 0:SLOTS] = cols_in[...]
     pl.semaphore_wait(barrier, len(partners))
 
     def first_way(c):
-        return 1 if c == 0 else -1
+        return 1 if c % 2 == 0 else -1
 
     def second_way(a):
         return 1 if a in (0, 1) else -1
@@ -234,6 +261,10 @@
         take(("g2r", c, 2), 2)
 
     def tables_0():
+        rows_got.wait()
+        cols_got.wait()
+        IX[0:1, 0:SLOTS] = RV[...]
+        IX[8:9, 0:SLOTS] = CV[...]
         lane = lax.broadcasted_iota(jnp.int32, (TILE, TILE), 1)
         down = lax.broadcasted_iota(jnp.int32, (TILE, TILE), 0)
         rows = jnp.broadcast_to(IX[0:1, :], (TILE, TILE))
@@ -268,7 +299,7 @@
             TV[at + 3 : at + 4, :] = jnp.where(any_own > 0, upto - 1, SLOTS)
 
     def tables_1():
-        copy = pltpu.make_async_copy(TV, TS, lsem.at[7])
+        copy = pltpu.make_async_copy(TV, TS, lsem.at[LOCAL])
         copy.start()
         copy.wait()
 
@@ -337,54 +368,39 @@
                 s = part * SLOTS_AT_ONCE + n * 4 + j
                 BT[s] = BK[s].T
 
-    gather_0(0)
-    gather_own(0)
-    gather_0(1)
-    tables_0()
-    blocks_in.wait()
-    turn_blocks(0)
-    tables_1()
-    gather_1(0)
-    gather_own(1)
-    gather_2(0)
-    turn_blocks(1)
-    gather_1(1)
-    gather_3(0)
-    gather_4(0)
-    turn_blocks(2)
-    gather_2(1)
-    gather_6(0)
-    gather_3(1)
-    gather_8(0)
-    multiply(0, 0)
-    gather_4(1)
-    multiply(0, 1)
-    multiply(0, 2)
-    reduce_0(0)
-    gather_6(1)
-    reduce_1(0)
-    reduce_2(0)
-    gather_8(1)
-    multiply(1, 0)
-    multiply(1, 1)
-    multiply(1, 2)
-    reduce_0(1)
-    reduce_3(0)
-    reduce_1(1)
-    reduce_2(1)
+    def run(order, table):
+        for name, *args in order:
+            table[name](*args)
+
+    def prepare():
+        tables_0()
+        blocks_in.wait()
+        turn_blocks(0)
+        tables_1()
+
+    def multiply_all(c):
+        gather_8(c)
+        for part in range(3):
+            multiply(c, part)
+        reduce_0(c)
+
+    steps = dict(g0=gather_0, own=gather_own, g1=gather_1, g2=gather_2, g3=gather_3, g4=gather_4)
+    steps.update(g6=gather_6, mm=multiply_all, r1=reduce_1, r2=reduce_2, r3=reduce_3)
+    steps.update(prep=prepare, turn=turn_blocks)
+    run(FORWARD, steps)
     weight_in.wait()
     ups_in.wait()
-    reduce_3(1)
 
     bias_rows = []
-    for n in range(CHUNKS):
-        columns = slice(n * WIDE, (n + 1) * WIDE)
-        pre = jnp.dot(HD[...], WT[:, columns], preferred_element_type=F32) + bias[:, columns]
+    bias_in.wait()
+    for n in range(2):
+        columns = slice(n * HALF, (n + 1) * HALF)
+        pre = jnp.dot(HD[...], WT[:, columns], preferred_element_type=F32) + BV[:, columns]
         sig = jax.nn.sigmoid(pre)
         AO[:, columns] = (pre * sig).astype(BF16)
         dpre = (UP[:, columns].astype(F32) * sig * (1.0 + pre * (1.0 - sig))).astype(BF16)
         DP[:, columns] = dpre
-        bias_rows.append(jnp.sum(dpre.astype(F32).reshape(32, 8, WIDE), axis=0))
+        bias_rows.append(jnp.sum(dpre.astype(F32).reshape(32, 8, HALF), axis=0))
 
     def hidden(c, place):
         return DG[c].at[pl.ds(2 * place, 2)]
@@ -432,7 +448,7 @@
                 GP[:, yy * SIDE + zz, :, 16:24, :] = jnp.broadcast_to(
                     sums, (2, SIDE, 8, TILE)
                 )
-        send(("wk",), GP.at[1 - k], AK, dev(dk=1), out=2)
+        send(("wk",), GP.at[1 - k], AK, dev(dk=1), out=CHUNKS + 0)
 
     def weight_1():
         wait_bytes(AK, rsem.at[groups[("wk",)]])
@@ -440,7 +456,7 @@
         PX[...] = AK[...].astype(BF16)
         for n, (dy, dz) in enumerate(plane):
             there = ((y + dy) % SIDE) * SIDE + (z + dz) % SIDE
-            send(("wp",), PX.at[there], PR.at[n], dev(dy=dy, dz=dz), out=3)
+            send(("wp",), PX.at[there], PR.at[n], dev(dy=dy, dz=dz), out=CHUNKS + 1)
 
     def weight_2():
         wait_bytes(PR, rsem.at[groups[("wp",)]])
@@ -449,7 +465,7 @@
             value = value + PR[n].astype(F32)
         XA[...] = value
         for n in (2, 1, 3):
-            send(("wx",), XA.at[(x + n) % SIDE], XB.at[n - 1], dev(dx=n), out=4)
+            send(("wx",), XA.at[(x + n) % SIDE], XB.at[n - 1], dev(dx=n), out=CHUNKS + 2)
 
     def weight_3():
         wait_bytes(XB, rsem.at[groups[("wx",)]])
@@ -459,17 +475,17 @@
         FK[k, x, ri] = (value * scale).astype(BF16)
         mine = FK.at[k, x, ri]
         for dy, dz in plane:
-            send(("vp",), mine, mine, dev(dy=dy, dz=dz), out=5)
+            send(("vp",), mine, mine, dev(dy=dy, dz=dz), out=CHUNKS + 3)
 
     def weight_4():
         wait_bytes(LIKE, rsem.at[groups[("vp",)]])
         mine = FK.at[k, x]
         for n in (2, 1, 3):
-            send(("vx",), mine, mine, dev(dx=n), out=6)
+            send(("vx",), mine, mine, dev(dx=n), out=CHUNKS + 4)
 
     def weight_5():
         wait_bytes(FK.at[0, pl.ds(0, 3)], rsem.at[groups[("vx",)]])
-        send(("vk",), FK.at[k], FK.at[k], dev(dk=1), out=7)
+        send(("vk",), FK.at[k], FK.at[k], dev(dk=1), out=CHUNKS + 5)
 
     def weight_6():
         wait_bytes(FK.at[0], rsem.at[groups[("vk",)]])
@@ -547,63 +563,15 @@
             value = value + SR[c, h, 4, 2].astype(F32)
             FO[h * TILE : (h + 1) * TILE, c * WIDE : (c + 1) * WIDE] = value.astype(BF16)
 
-    out = []
-
-    def leave(src, dst):
-        copy = pltpu.make_async_copy(src, dst, lsem.at[8 + len(out)])
-        copy.start()
-        out.append(copy)
-
-    spread_0(0)
-    weight_0()
-    leave(AO, act_o)
-    spread_1(0)
-    spread_0(1)
-    weight_1()
-    spread_2(0)
-    spread_3(0)
-    for part in range(3):
-        multiply_back(0, part)
-    for i in range(4):
-        back_0(0, i)
-    spread_1(1)
-    weight_2()
-    spread_2(1)
-    back_1(0, 0)
-    back_1(0, 1)
-    spread_3(1)
-    for part in range(3):
-        multiply_back(1, part)
-    back_0(1, 0)
-    back_1(0, 2)
-    back_0(1, 1)
-    back_2(0, 0)
-    back_1(0, 3)
-    back_0(1, 2)
-    back_2(0, 1)
-    back_0(1, 3)
-    weight_3()
-    back_1(1, 0)
-    back_2(0, 2)
-    back_2(0, 3)
-    back_1(1, 1)
-    back_1(1, 2)
-    back_3(0)
-    leave(FO.at[:, pl.ds(0, WIDE)], gf_o.at[:, pl.ds(0, WIDE)])
-    back_2(1, 0)
-    back_1(1, 3)
-    weight_4()
-    back_2(1, 1)
-    back_2(1, 2)
-    back_2(1, 3)
-    weight_5()
-    weight_6()
-    leave(WO, gw_o)
-    leave(BO, gb_o)
-    back_3(1)
-    leave(FO.at[:, pl.ds(WIDE, WIDE)], gf_o.at[:, pl.ds(WIDE, WIDE)])
-    for copy in out:
-        copy.wait()
+    def multiply_back_all(c):
+        spread_3(c)
+        for part in range(3):
+            multiply_back(c, part)
+
+    steps = dict(w0=weight_0, w1=weight_1, w2=weight_2, w3=weight_3, w4=weight_4, w5=weight_5)
+    steps.update(w6=weight_6, s0=spread_0, s1=spread_1, s2=spread_2, mm=multiply_back_all)
+    steps.update(b0=back_0, b1=back_1, b2=back_2, b3=back_3)
+    run(BACKWARD, steps)
 
     assert len(groups) == GROUPS, len(groups)
     for c in range(CHUNKS):
@@ -614,23 +582,19 @@
         wait_bytes(like, ssem.at[number])
 
 
-def finish_kernel(a, b, c, d, ao, bo, co, do, av, bv, cv, dv, sem):
-    pairs = ((c, cv, co), (a, av, ao), (b, bv, bo), (d, dv, do))
-    copies_in = [pltpu.make_async_copy(p[0], p[1], sem.at[n]) for n, p in enumerate(pairs)]
-    copies_out = [pltpu.make_async_copy(p[1], p[2], sem.at[4 + n]) for n, p in enumerate(pairs)]
-    for copy in copies_in:
+def finish_kernel(a, b, c, d, ao, bo, co, do, sem):
+    pairs = ((c, co), (a, ao), (b, bo), (d, do))
+    copies = [pltpu.make_async_copy(p[0], p[1], sem.at[n]) for n, p in enumerate(pairs)]
+    for copy in copies:
         copy.start()
-    for copy_in, copy_out in zip(copies_in, copies_out):
-        copy_in.wait()
-        copy_out.start()
-    for copy in copies_out:
+    for copy in copies:
         copy.wait()
 
 
 def shards(features, blocks, block_rows, block_cols, block_count, weight, bias_vector, upstream):
     scale = 1.0 / math.sqrt(features.shape[0] * SIDE * SIDE * SIDE * 2)
     vmem = pl.BlockSpec(memory_space=pltpu.VMEM)
-    hbm = pl.BlockSpec(memory_space=pl.ANY)
+    hbm = pl.BlockSpec(memory_space=pltpu.HBM)
     smem = pl.BlockSpec(memory_space=pltpu.SMEM)
     shapes = (
         jax.ShapeDtypeStruct((256, 512), BF16),
@@ -641,25 +605,22 @@
     results = pl.pallas_call(
         functools.partial(step_kernel, scale),
         out_shape=shapes,
-        in_specs=[smem, vmem, vmem, hbm, hbm, hbm, vmem, hbm],
-        out_specs=(hbm, hbm, hbm, hbm),
+        in_specs=[smem] + [hbm] * 7,
+        out_specs=(vmem, vmem, vmem, vmem),
         scratch_shapes=[
-            pltpu.VMEM((KBLOCKS, TILE, WIDE), BF16),
-            pltpu.VMEM((KBLOCKS, TILE, WIDE), BF16),
+            *[pltpu.VMEM((KBLOCKS, TILE, WIDE), BF16)] * CHUNKS,
+            *[pltpu.VMEM((SLOTS + 1, TILE, WIDE), F32)] * CHUNKS,
+            *[pltpu.VMEM((IBLOCKS, TILE, WIDE), BF16)] * CHUNKS,
             pltpu.VMEM((SLOTS, TILE, TILE), BF16),
             pltpu.VMEM((SLOTS, TILE, TILE), BF16),
             pltpu.VMEM((512, 512), BF16),
             pltpu.VMEM((256, 512), BF16),
-            pltpu.VMEM((SLOTS + 1, TILE, WIDE), F32),
-            pltpu.VMEM((SLOTS + 1, TILE, WIDE), F32),
             pltpu.VMEM((CHUNKS, SIDE, 256, WIDE), BF16),
             pltpu.VMEM((CHUNKS, SIDE, 256, WIDE), BF16),
             pltpu.VMEM((CHUNKS, 3, 256, WIDE), BF16),
             pltpu.VMEM((CHUNKS, 3, 256, WIDE), BF16),
             pltpu.VMEM((256, 512), BF16),
             pltpu.VMEM((256, 512), BF16),
-            pltpu.VMEM((IBLOCKS, TILE, WIDE), BF16),
-            pltpu.VMEM((IBLOCKS, TILE, WIDE), BF16),
             pltpu.VMEM((CHUNKS, 2, TILE, WIDE), F32),
             pltpu.VMEM((CHUNKS, 2, 5, 3, TILE, WIDE), BF16),
             pltpu.VMEM((CHUNKS, 2, 5, 3, TILE, WIDE), BF16),
@@ -671,39 +632,42 @@
             pltpu.VMEM((3, 24, TILE), F32),
             pltpu.VMEM((2, SIDE, 16, 24, TILE), BF16),
             pltpu.VMEM((15, 24, TILE), BF16),
-            pltpu.VMEM((256, 512), BF16),
-            pltpu.VMEM((256, 512), BF16),
-            pltpu.VMEM((512, 512), F32),
+            pltpu.VMEM((1, SLOTS), jnp.int32),
+            pltpu.VMEM((1, SLOTS), jnp.int32),
             pltpu.VMEM((1, 512), F32),
             pltpu.VMEM((16, TILE), jnp.int32),
             pltpu.VMEM((16, TILE), jnp.int32),
             pltpu.SMEM((16, TILE), jnp.int32),
-            pltpu.SemaphoreType.DMA((13,)),
+            pltpu.SemaphoreType.DMA((LOCAL + 1,)),
             pltpu.SemaphoreType.DMA((CHUNKS + 6,)),
             pltpu.SemaphoreType.DMA((GROUPS,)),
         ],
         compiler_params=pltpu.CompilerParams(
-            collective_id=0, has_side_effects=True, vmem_limit_bytes=60 * 2**20
+            collective_id=0, has_side_effects=True, vmem_limit_bytes=46 * 2**20
         ),
         name="graph_layer",
     )(
         block_count,
-        block_rows[0],
-        block_cols[0],
-        features,
-        blocks[0, 0],
-        weight,
-        bias_vector.reshape(1, 512),
-        upstream,
+        *[
+            pltpu.with_memory_space_constraint(array, pltpu.HBM)
+            for array in (
+                block_rows[0],
+                block_cols[0],
+                features,
+                blocks[0, 0],
+                weight,
+                bias_vector.reshape(1, 512),
+                upstream,
+            )
+        ],
     )
     activated, grad_features, grad_weight, grad_bias = pl.pallas_call(
         finish_kernel,
         out_shape=shapes,
-        in_specs=[hbm] * 4,
+        in_specs=[vmem] * 4,
         out_specs=(hbm,) * 4,
-        scratch_shapes=[pltpu.VMEM(s.shape, s.dtype) for s in shapes]
-        + [pltpu.SemaphoreType.DMA((8,))],
-        compiler_params=pltpu.CompilerParams(vmem_limit_bytes=60 * 2**20),
+        scratch_shapes=[pltpu.SemaphoreType.DMA((4,))],
+        compiler_params=pltpu.CompilerParams(vmem_limit_bytes=2 * 2**20),
         name="finish",
     )(*results)
     return (activated, grad_weight, grad_bias.reshape(512), grad_features)

time: 94.2 us -> 86 us (0.913)
  Pallas kernels: 91.5 us -> 84.2 us
    pallas_call x1, Pallas kernels: 89.1 us -> 83.1 us  [shards(): pl.pallas_call(functools.partial(step_kernel, scale), out_shape=shapes, i...]
    pallas_call x1, Pallas kernels: 2.43 us -> 1.17 us  [shards(): pl.pallas_call(finish_kernel, out_shape=shapes, in_specs=[vmem] * 4, out_...]
where the time goes in v3:
time: 86 us; the launch traced here: 85.5 us
  Pallas kernels  84.2 us (98%)
  between operations  1.29 us (2%)
    pallas_call x1, Pallas kernels, shards(): pl.pallas_call(functools.partial(step_kernel, scale), out_shape=shapes, i...  83.1 us

profile of v3, /device:TPU:0, one launch (start us, length us, event | category | flops | bytes accessed | tf_op | source)
XLA Modules:
  0.0 85.5 jit_solution(5214136122959806155)
XLA Ops:
  1.3 83.1 %graph_layer.1 = (bf16[256,512]{1,0:T(8,128)(2,1)S(1)}, bf16[256,512]{1,0:T(8,128)(2,1)S(1)}, f32[512,512]{1,0:T(8,128)S(1)}, f32[1,512]{1,0:T(1,128)S(1)}) custom-call(s32[1,1]{1,0:T(1,128)S(6)} %copy.12.count, s32[1,48]{1,0:T(1,128)} %bitcast.7, s32[1,48]{1,0:T(1,128)} %bitcast.8, bf16[256,512]{1,0:T(8,128)(2,1)} %feat.1, bf16[48,128,128]{2,1,0:T(8,128)(2,1)} %bitcast.5, ...), custom_call_target="tpu_custom_call" | custom-call | tf_op jit(solution)/shard_map/graph_layer/pallas_call | solution.py:605
  84.3 1.2 %finish.1 = (bf16[256,512]{1,0:T(8,128)(2,1)}, bf16[256,512]{1,0:T(8,128)(2,1)}, f32[512,512]{1,0:T(8,128)}, f32[1,512]{1,0:T(1,128)}) custom-call(bf16[256,512]{1,0:T(8,128)(2,1)S(1)} %get-tuple-element.12.a, bf16[256,512]{1,0:T(8,128)(2,1)S(1)} %get-tuple-element.13.b, f32[512,512]{1,0:T(8,128)S(1)} %get-tuple-element.14.c, f32[1,512]{1,0:T(1,128)S(1)} %get-tuple-element.15.d), custom_call_target="tpu_custom_call" | custom-call | tf_op jit(solution)/shard_map/finish/pallas_call | solution.py:664

commit v4 on v3

--- a/solution.py
+++ b/solution.py
@@ -13,8 +13,11 @@
 BF16 = jnp.bfloat16
 SIDE = 4
 TILE = 128
-WIDE = 256
-CHUNKS = 2
+WIDTHS = (256, 128, 128)
+STARTS = (0, 256, 384)
+CHUNKS = len(WIDTHS)
+DIRECT_SUMS = (1, 2)
+DIRECT_SPREAD = (1, 2)
 HALF = 256
 KBLOCKS = 32
 IBLOCKS = 16
@@ -23,76 +26,104 @@
 LOCAL = 2 * CHUNKS + 6
 FORWARD = (
     ("g0", 0),
+    ("g0", 2),
     ("own", 0),
-    ("g0", 1),
     ("prep",),
     ("g1", 0),
+    ("g0", 1),
+    ("turn", 1),
+    ("turn", 2),
+    ("g3", 0),
+    ("g1", 2),
+    ("g2", 0),
+    ("g4", 0),
+    ("g6", 0),
+    ("own", 2),
+    ("g3", 2),
+    ("g1", 1),
+    ("g4", 2),
+    ("mm", 0),
+    ("g6", 2),
     ("own", 1),
-    ("g2", 0),
-    ("turn", 1),
-    ("g1", 1),
-    ("g3", 0),
-    ("g4", 0),
+    ("g2", 2),
+    ("g3", 1),
+    ("g4", 1),
+    ("r1", 0),
+    ("mm", 2),
     ("g2", 1),
-    ("g3", 1),
-    ("turn", 2),
-    ("g6", 0),
-    ("g4", 1),
+    ("r2", 2),
     ("g6", 1),
-    ("mm", 0),
-    ("r1", 0),
+    ("r2", 0),
+    ("r1", 2),
     ("mm", 1),
-    ("r2", 0),
     ("r1", 1),
     ("r3", 0),
     ("r2", 1),
+    ("r3", 2),
     ("r3", 1),
 )
 BACKWARD = (
+    ("s0", 1),
+    ("w0",),
+    ("s0", 2),
     ("s0", 0),
-    ("w0",),
+    ("s2", 1),
+    ("w1",),
+    ("s1", 1),
+    ("s2", 2),
+    ("mm", 1),
+    ("s1", 2),
+    ("b0", 1, 0),
+    ("b0", 1, 3),
+    ("b0", 1, 2),
+    ("b0", 1, 1),
     ("s1", 0),
-    ("s0", 1),
-    ("w1",),
+    ("mm", 2),
+    ("b0", 2, 3),
+    ("w2",),
+    ("b0", 2, 1),
+    ("b0", 2, 0),
+    ("b1", 1, 2),
+    ("b0", 2, 2),
+    ("b1", 1, 3),
     ("s2", 0),
+    ("b1", 1, 0),
+    ("w3",),
+    ("b1", 1, 1),
     ("mm", 0),
     ("b0", 0, 0),
+    ("b0", 0, 2),
     ("b0", 0, 1),
-    ("b0", 0, 2),
+    ("b1", 2, 1),
+    ("w4",),
+    ("b1", 0, 0),
+    ("b2", 1, 0),
+    ("b1", 2, 2),
+    ("b1", 2, 0),
+    ("b2", 1, 2),
+    ("b1", 0, 2),
+    ("b1", 0, 1),
     ("b0", 0, 3),
-    ("s1", 1),
-    ("w2",),
-    ("s2", 1),
-    ("b1", 0, 0),
-    ("b1", 0, 1),
-    ("mm", 1),
-    ("b0", 1, 0),
-    ("b1", 0, 2),
-    ("b0", 1, 1),
+    ("b2", 0, 0),
+    ("b1", 2, 3),
+    ("b2", 2, 0),
+    ("b2", 1, 3),
+    ("w5",),
+    ("b2", 2, 2),
+    ("b2", 1, 1),
     ("b1", 0, 3),
-    ("w3",),
-    ("b2", 0, 0),
-    ("b0", 1, 2),
-    ("b0", 1, 3),
-    ("b1", 1, 0),
     ("b2", 0, 2),
-    ("b1", 1, 1),
     ("b2", 0, 1),
-    ("b1", 1, 2),
-    ("w4",),
-    ("b2", 1, 0),
-    ("b1", 1, 3),
+    ("b2", 2, 1),
+    ("b2", 2, 3),
+    ("b3", 1),
     ("b2", 0, 3),
-    ("b2", 1, 2),
-    ("b2", 1, 1),
+    ("w6",),
     ("b3", 0),
-    ("w5",),
-    ("b2", 1, 3),
-    ("w6",),
-    ("b3", 1),
+    ("b3", 2),
 )
 FAR = 1 << 17
-GROUPS = 41 * CHUNKS + 6
+GROUPS = 41 * CHUNKS + 6 - len(DIRECT_SUMS) - len(DIRECT_SPREAD)
 
 
 def wrap(value):
@@ -108,10 +139,12 @@
 def step_kernel(scale, count, rows_in, cols_in, feat, blocks, weight, bias, ups, *refs):
     AO, FO, WO, BO = refs[:4]
     refs = refs[4:]
-    G, Z, DG = refs[:CHUNKS], refs[CHUNKS : 2 * CHUNKS], refs[2 * CHUNKS : 3 * CHUNKS]
-    BK, BT, WT, UP, S1, R0, XS, XR, HD, DP, UK, SB, SR = refs[3 * CHUNKS : 3 * CHUNKS + 13]
-    GP, AK, PX, PR, XA, XB, FK, LIKE = refs[3 * CHUNKS + 13 : 3 * CHUNKS + 21]
-    RV, CV, BV, IX, TV, TS, lsem, ssem, rsem = refs[3 * CHUNKS + 21 :]
+    by_chunk = [refs[n * CHUNKS : (n + 1) * CHUNKS] for n in range(10)]
+    G, Z, DG, S1, R0, XS, XR, UK, SB, SR = by_chunk
+    refs = refs[10 * CHUNKS :]
+    BK, BT, WT, UP, HD, DP = refs[:6]
+    GP, AK, PX, PR, XA, XB, FK, LIKE = refs[6:14]
+    RV, CV, BV, IX, TV, TS, lsem, ssem, rsem = refs[14:]
     ri = lax.axis_index("row")
     ci = lax.axis_index("col")
     y, z = ri // SIDE, ri % SIDE
@@ -158,7 +191,7 @@
     own = [
         [
             fetch(
-                feat.at[pl.ds(h * TILE, TILE), pl.ds(c * WIDE, WIDE)],
+                feat.at[pl.ds(h * TILE, TILE), pl.ds(STARTS[c], WIDTHS[c])],
                 G[c].at[at_k(h, 0, 0)],
             )
             for h in range(2)
@@ -179,12 +212,12 @@
     for partner in partners:
         pl.semaphore_signal(barrier, inc=1, device_id=partner, device_id_type=MESH)
     for c in range(CHUNKS):
-        Z[c][SLOTS] = jnp.zeros((TILE, WIDE), F32)
+        Z[c][SLOTS] = jnp.zeros((TILE, WIDTHS[c]), F32)
     IX[...] = jnp.zeros_like(IX)
     pl.semaphore_wait(barrier, len(partners))
 
     def first_way(c):
-        return 1 if c % 2 == 0 else -1
+        return (1, -1, -1)[c]
 
     def second_way(a):
         return 1 if a in (0, 1) else -1
@@ -328,38 +361,49 @@
 
     def reduce_0(c):
         for dx in (2, 3, 1, 0):
-            S1[c, dx] = part_of(c, 1, dx).astype(BF16)
+            S1[c][dx] = part_of(c, 1, dx).astype(BF16)
             mirrored = wrap(-dx)
-            send(("c0", c, mirrored), S1.at[c, dx], R0.at[c, mirrored], dev(dk=1))
+            send(("c0", c, mirrored), S1[c].at[dx], R0[c].at[mirrored], dev(dk=1))
 
     def paired(c, dx):
         take(("c0", c, dx), 2)
-        return part_of(c, 0, dx) + R0[c, dx].astype(F32)
+        return part_of(c, 0, dx) + R0[c][dx].astype(F32)
 
     def reduce_1(c):
-        XS[c, 0] = paired(c, 2).astype(BF16)
-        for half in range(2):
-            lines = pl.ds(half * TILE, TILE)
-            send(("cf", c, half), XS.at[c, 0, lines], XR.at[c, 0, lines], dev(dx=turn))
-        XS[c, 1] = paired(c, 3).astype(BF16)
-        send(("cd", c), XS.at[c, 1], XR.at[c, 1], dev(dx=-turn))
+        XS[c][0] = paired(c, 2).astype(BF16)
+        if c in DIRECT_SUMS:
+            send(("cf", c), XS[c].at[0], XR[c].at[0], dev(dx=2))
+        else:
+            for half in range(2):
+                lines = pl.ds(half * TILE, TILE)
+                send(("cf", c, half), XS[c].at[0, lines], XR[c].at[0, lines], dev(dx=turn))
+        XS[c][1] = paired(c, 3).astype(BF16)
+        send(("cd", c), XS[c].at[1], XR[c].at[1], dev(dx=-turn))
+        if c in DIRECT_SUMS:
+            XS[c][2] = paired(c, 1).astype(BF16)
+            send(("cr", c), XS[c].at[2], XR[c].at[2], dev(dx=turn))
 
     def reduce_2(c):
+        if c in DIRECT_SUMS:
+            return
         value = paired(c, 1)
         for half in range(2):
             lines = pl.ds(half * TILE, TILE)
             part = value[half * TILE : (half + 1) * TILE]
             take(("cf", c, half), 1)
-            XS[c, 2, lines] = (part + XR[c, 0, lines].astype(F32)).astype(BF16)
-            send(("cr", c), XS.at[c, 2, lines], XR.at[c, 2, lines], dev(dx=turn))
+            XS[c][2, lines] = (part + XR[c][0, lines].astype(F32)).astype(BF16)
+            send(("cr", c), XS[c].at[2, lines], XR[c].at[2, lines], dev(dx=turn))
 
     def reduce_3(c):
         value = paired(c, 0)
         take(("cd", c), 2)
-        value = value + XR[c, 1].astype(F32)
+        value = value + XR[c][1].astype(F32)
         take(("cr", c), 2)
-        value = value + XR[c, 2].astype(F32)
-        HD[:, c * WIDE : (c + 1) * WIDE] = value.astype(BF16)
+        value = value + XR[c][2].astype(F32)
+        if c in DIRECT_SUMS:
+            take(("cf", c), 2)
+            value = value + XR[c][0].astype(F32)
+        HD[:, STARTS[c] : STARTS[c] + WIDTHS[c]] = value.astype(BF16)
 
     def turn_blocks(part):
         @pl.loop(0, SLOTS_AT_ONCE // 4)
@@ -408,20 +452,27 @@
     def spread_0(c):
         value = lax.dot_general(
             DP[...],
-            WT[pl.ds(c * WIDE, WIDE), :],
+            WT[pl.ds(STARTS[c], WIDTHS[c]), :],
             (((1,), (1,)), ((), ())),
             preferred_element_type=F32,
         )
-        DG[c][0:2] = value.astype(BF16).reshape(2, TILE, WIDE)
-        for half in range(2):
-            send(("sp", c, half), DG[c].at[half], DG[c].at[6 + half], dev(dx=turn))
+        DG[c][0:2] = value.astype(BF16).reshape(2, TILE, WIDTHS[c])
+        if c in DIRECT_SPREAD:
+            send(("sr", c), hidden(c, 0), hidden(c, 2), dev(dx=2))
+            send(("sp", c), hidden(c, 0), hidden(c, 3), dev(dx=turn))
+        else:
+            for half in range(2):
+                send(("sp", c, half), DG[c].at[half], DG[c].at[6 + half], dev(dx=turn))
         send(("sm", c), hidden(c, 0), hidden(c, 1), dev(dx=-turn))
         send(("sc", c), hidden(c, 0), hidden(c, SIDE), dev(dk=1))
 
     def spread_1(c):
-        for half in range(2):
-            take(("sp", c, half), 1)
-            send(("sr", c), DG[c].at[6 + half], DG[c].at[4 + half], dev(dx=turn))
+        if c in DIRECT_SPREAD:
+            take(("sp", c), 2)
+        else:
+            for half in range(2):
+                take(("sp", c, half), 1)
+                send(("sr", c), DG[c].at[6 + half], DG[c].at[4 + half], dev(dx=turn))
         send(("sc", c), hidden(c, 3), hidden(c, SIDE + 1), dev(dk=1))
         take(("sm", c), 2)
         send(("sc", c), hidden(c, 1), hidden(c, SIDE + 3), dev(dk=1))
@@ -519,19 +570,19 @@
         name = NAMES[i]
         a, e = offset(c, name), group_way(name)
         for h in range(2):
-            SB[c, h, i, 0] = sum_of(c, h, a, 2).astype(BF16)
-            send(("bf", c, i), SB.at[c, h, i, 0], SR.at[c, h, i, 0], along(h, False, e))
-        for h in range(2):
-            SB[c, h, i, 1] = sum_of(c, h, a, -e).astype(BF16)
-            send(("bd", c, i), SB.at[c, h, i, 1], SR.at[c, h, i, 1], along(h, False, -e))
+            SB[c][h, i, 0] = sum_of(c, h, a, 2).astype(BF16)
+            send(("bf", c, i), SB[c].at[h, i, 0], SR[c].at[h, i, 0], along(h, False, e))
+        for h in range(2):
+            SB[c][h, i, 1] = sum_of(c, h, a, -e).astype(BF16)
+            send(("bd", c, i), SB[c].at[h, i, 1], SR[c].at[h, i, 1], along(h, False, -e))
 
     def back_1(c, i):
         name = NAMES[i]
         a, e = offset(c, name), group_way(name)
         take(("bf", c, i), 2)
         for h in range(2):
-            SB[c, h, i, 2] = (sum_of(c, h, a, e) + SR[c, h, i, 0].astype(F32)).astype(BF16)
-            send(("br", c, i), SB.at[c, h, i, 2], SR.at[c, h, i, 2], along(h, False, e))
+            SB[c][h, i, 2] = (sum_of(c, h, a, e) + SR[c][h, i, 0].astype(F32)).astype(BF16)
+            send(("br", c, i), SB[c].at[h, i, 2], SR[c].at[h, i, 2], along(h, False, e))
 
     def back_2(c, i):
         name = NAMES[i]
@@ -541,27 +592,27 @@
         if name == "relay":
             take(("tf", c), 2)
         for h in range(2):
-            value = sum_of(c, h, offset(c, name), 0) + SR[c, h, i, 1].astype(F32)
-            value = value + SR[c, h, i, 2].astype(F32)
+            value = sum_of(c, h, offset(c, name), 0) + SR[c][h, i, 1].astype(F32)
+            value = value + SR[c][h, i, 2].astype(F32)
             if name == "far":
-                SB[c, h, 4, 0] = value.astype(BF16)
-                send(("tf", c), SB.at[c, h, 4, 0], SR.at[c, h, 4, 0], along(h, True, e))
+                SB[c][h, 4, 0] = value.astype(BF16)
+                send(("tf", c), SB[c].at[h, 4, 0], SR[c].at[h, 4, 0], along(h, True, e))
             elif name == "near":
-                SB[c, h, 4, 1] = value.astype(BF16)
-                send(("td", c), SB.at[c, h, 4, 1], SR.at[c, h, 4, 1], along(h, True, -e))
+                SB[c][h, 4, 1] = value.astype(BF16)
+                send(("td", c), SB[c].at[h, 4, 1], SR[c].at[h, 4, 1], along(h, True, -e))
             elif name == "relay":
-                SB[c, h, 4, 2] = (value + SR[c, h, 4, 0].astype(F32)).astype(BF16)
-                send(("tr", c), SB.at[c, h, 4, 2], SR.at[c, h, 4, 2], along(h, True, e))
+                SB[c][h, 4, 2] = (value + SR[c][h, 4, 0].astype(F32)).astype(BF16)
+                send(("tr", c), SB[c].at[h, 4, 2], SR[c].at[h, 4, 2], along(h, True, e))
             else:
-                UK[c, h] = value
+                UK[c][h] = value
 
     def back_3(c):
         take(("td", c), 2)
         take(("tr", c), 2)
         for h in range(2):
-            value = UK[c, h] + SR[c, h, 4, 1].astype(F32)
-            value = value + SR[c, h, 4, 2].astype(F32)
-            FO[h * TILE : (h + 1) * TILE, c * WIDE : (c + 1) * WIDE] = value.astype(BF16)
+            value = UK[c][h] + SR[c][h, 4, 1].astype(F32)
+            value = value + SR[c][h, 4, 2].astype(F32)
+            FO[h * TILE : (h + 1) * TILE, STARTS[c] : STARTS[c] + WIDTHS[c]] = value.astype(BF16)
 
     def multiply_back_all(c):
         spread_3(c)
@@ -608,22 +659,22 @@
         in_specs=[smem] + [hbm] * 7,
         out_specs=(vmem, vmem, vmem, vmem),
         scratch_shapes=[
-            *[pltpu.VMEM((KBLOCKS, TILE, WIDE), BF16)] * CHUNKS,
-            *[pltpu.VMEM((SLOTS + 1, TILE, WIDE), F32)] * CHUNKS,
-            *[pltpu.VMEM((IBLOCKS, TILE, WIDE), BF16)] * CHUNKS,
+            *[pltpu.VMEM((KBLOCKS, TILE, w), BF16) for w in WIDTHS],
+            *[pltpu.VMEM((SLOTS + 1, TILE, w), F32) for w in WIDTHS],
+            *[pltpu.VMEM((IBLOCKS, TILE, w), BF16) for w in WIDTHS],
+            *[pltpu.VMEM((SIDE, 256, w), BF16) for w in WIDTHS],
+            *[pltpu.VMEM((SIDE, 256, w), BF16) for w in WIDTHS],
+            *[pltpu.VMEM((3, 256, w), BF16) for w in WIDTHS],
+            *[pltpu.VMEM((3, 256, w), BF16) for w in WIDTHS],
+            *[pltpu.VMEM((2, TILE, w), F32) for w in WIDTHS],
+            *[pltpu.VMEM((2, 5, 3, TILE, w), BF16) for w in WIDTHS],
+            *[pltpu.VMEM((2, 5, 3, TILE, w), BF16) for w in WIDTHS],
             pltpu.VMEM((SLOTS, TILE, TILE), BF16),
             pltpu.VMEM((SLOTS, TILE, TILE), BF16),
             pltpu.VMEM((512, 512), BF16),
             pltpu.VMEM((256, 512), BF16),
-            pltpu.VMEM((CHUNKS, SIDE, 256, WIDE), BF16),
-            pltpu.VMEM((CHUNKS, SIDE, 256, WIDE), BF16),
-            pltpu.VMEM((CHUNKS, 3, 256, WIDE), BF16),
-            pltpu.VMEM((CHUNKS, 3, 256, WIDE), BF16),
             pltpu.VMEM((256, 512), BF16),
             pltpu.VMEM((256, 512), BF16),
-            pltpu.VMEM((CHUNKS, 2, TILE, WIDE), F32),
-            pltpu.VMEM((CHUNKS, 2, 5, 3, TILE, WIDE), BF16),
-            pltpu.VMEM((CHUNKS, 2, 5, 3, TILE, WIDE), BF16),
             pltpu.VMEM((2, 16, SIDE, 24, TILE), F32),
             pltpu.VMEM((16, SIDE, 24, TILE), F32),
             pltpu.VMEM((16, SIDE, 24, TILE), BF16),

time: 86 us -> 79.4 us (0.923)
  Pallas kernels: 84.2 us -> 78 us
    pallas_call x1, Pallas kernels: 83.1 us -> 76.8 us  [shards(): pl.pallas_call(functools.partial(step_kernel, scale), out_shape=shapes, i...]
where the time goes in v4:
time: 79.4 us; the launch traced here: 79.3 us
  Pallas kernels  78 us (98%)
  between operations  1.29 us (2%)
    pallas_call x1, Pallas kernels, shards(): pl.pallas_call(functools.partial(step_kernel, scale), out_shape=shapes, i...  76.8 us

profile of v4, /device:TPU:0, one launch (start us, length us, event | category | flops | bytes accessed | tf_op | source)
XLA Modules:
  0.0 79.3 jit_solution(10951613931633546953)
XLA Ops:
  1.3 76.8 %graph_layer.1 = (bf16[256,512]{1,0:T(8,128)(2,1)S(1)}, bf16[256,512]{1,0:T(8,128)(2,1)S(1)}, f32[512,512]{1,0:T(8,128)S(1)}, f32[1,512]{1,0:T(1,128)S(1)}) custom-call(s32[1,1]{1,0:T(1,128)S(6)} %copy.12.count, s32[1,48]{1,0:T(1,128)} %bitcast.7, s32[1,48]{1,0:T(1,128)} %bitcast.8, bf16[256,512]{1,0:T(8,128)(2,1)} %feat.1, bf16[48,128,128]{2,1,0:T(8,128)(2,1)} %bitcast.5, ...), custom_call_target="tpu_custom_call" | custom-call | tf_op jit(solution)/shard_map/graph_layer/pallas_call | solution.py:656
  78.1 1.2 %finish.1 = (bf16[256,512]{1,0:T(8,128)(2,1)}, bf16[256,512]{1,0:T(8,128)(2,1)}, f32[512,512]{1,0:T(8,128)}, f32[1,512]{1,0:T(1,128)}) custom-call(bf16[256,512]{1,0:T(8,128)(2,1)S(1)} %get-tuple-element.12.a, bf16[256,512]{1,0:T(8,128)(2,1)S(1)} %get-tuple-element.13.b, f32[512,512]{1,0:T(8,128)S(1)} %get-tuple-element.14.c, f32[1,512]{1,0:T(1,128)S(1)} %get-tuple-element.15.d), custom_call_target="tpu_custom_call" | custom-call | tf_op jit(solution)/shard_map/finish/pallas_call | solution.py:715

commit v5 on v4

--- a/solution.py
+++ b/solution.py
@@ -13,11 +13,12 @@
 BF16 = jnp.bfloat16
 SIDE = 4
 TILE = 128
-WIDTHS = (256, 128, 128)
-STARTS = (0, 256, 384)
+WIDTHS = (128, 128, 128, 128)
+STARTS = (0, 128, 256, 384)
 CHUNKS = len(WIDTHS)
-DIRECT_SUMS = (1, 2)
-DIRECT_SPREAD = (1, 2)
+DIRECT_SUMS = (2, 3)
+DIRECT_SPREAD = (0, 1, 2, 3)
+DIRECT_LAST = ()
 HALF = 256
 KBLOCKS = 32
 IBLOCKS = 16
@@ -26,104 +27,132 @@
 LOCAL = 2 * CHUNKS + 6
 FORWARD = (
     ("g0", 0),
+    ("g0", 1),
+    ("own", 0),
+    ("own", 1),
+    ("prep",),
     ("g0", 2),
-    ("own", 0),
-    ("prep",),
     ("g1", 0),
-    ("g0", 1),
+    ("g1", 1),
+    ("g2", 0),
     ("turn", 1),
-    ("turn", 2),
     ("g3", 0),
     ("g1", 2),
-    ("g2", 0),
+    ("g0", 3),
+    ("g2", 1),
+    ("turn", 2),
+    ("g3", 1),
     ("g4", 0),
+    ("own", 2),
     ("g6", 0),
-    ("own", 2),
+    ("g4", 1),
     ("g3", 2),
-    ("g1", 1),
-    ("g4", 2),
+    ("g6", 1),
+    ("g1", 3),
     ("mm", 0),
     ("g6", 2),
-    ("own", 1),
     ("g2", 2),
-    ("g3", 1),
-    ("g4", 1),
+    ("g4", 2),
+    ("g3", 3),
+    ("mm", 1),
+    ("own", 3),
+    ("g4", 3),
     ("r1", 0),
     ("mm", 2),
-    ("g2", 1),
-    ("r2", 2),
-    ("g6", 1),
+    ("r1", 1),
+    ("g6", 3),
+    ("g2", 3),
     ("r2", 0),
     ("r1", 2),
-    ("mm", 1),
-    ("r1", 1),
+    ("mm", 3),
+    ("r2", 1),
+    ("r2", 2),
+    ("r1", 3),
+    ("r3", 1),
     ("r3", 0),
-    ("r2", 1),
     ("r3", 2),
-    ("r3", 1),
+    ("r2", 3),
+    ("r3", 3),
 )
 BACKWARD = (
+    ("s0", 0),
+    ("w0",),
     ("s0", 1),
-    ("w0",),
+    ("w1",),
+    ("s2", 0),
+    ("s1", 0),
+    ("s0", 3),
+    ("mm", 0),
+    ("s2", 1),
+    ("b0", 0, 3),
+    ("s1", 1),
+    ("b0", 0, 2),
     ("s0", 2),
-    ("s0", 0),
-    ("s2", 1),
-    ("w1",),
-    ("s1", 1),
+    ("b0", 0, 1),
+    ("b0", 0, 0),
+    ("mm", 1),
+    ("b0", 1, 2),
+    ("s2", 3),
+    ("b0", 1, 0),
+    ("s1", 3),
+    ("b0", 1, 1),
+    ("b0", 1, 3),
+    ("b1", 0, 2),
+    ("w2",),
+    ("mm", 3),
     ("s2", 2),
-    ("mm", 1),
+    ("b0", 3, 3),
     ("s1", 2),
-    ("b0", 1, 0),
-    ("b0", 1, 3),
-    ("b0", 1, 2),
-    ("b0", 1, 1),
-    ("s1", 0),
-    ("mm", 2),
-    ("b0", 2, 3),
-    ("w2",),
-    ("b0", 2, 1),
-    ("b0", 2, 0),
     ("b1", 1, 2),
-    ("b0", 2, 2),
-    ("b1", 1, 3),
-    ("s2", 0),
+    ("b0", 3, 2),
+    ("b0", 3, 0),
     ("b1", 1, 0),
     ("w3",),
-    ("b1", 1, 1),
-    ("mm", 0),
-    ("b0", 0, 0),
-    ("b0", 0, 2),
-    ("b0", 0, 1),
-    ("b1", 2, 1),
-    ("w4",),
+    ("mm", 2),
+    ("b0", 2, 0),
+    ("b0", 2, 2),
+    ("b0", 2, 1),
+    ("b1", 3, 2),
+    ("b0", 2, 3),
+    ("b1", 0, 3),
+    ("b1", 2, 0),
     ("b1", 0, 0),
     ("b2", 1, 0),
+    ("b1", 3, 0),
+    ("b0", 3, 1),
     ("b1", 2, 2),
-    ("b1", 2, 0),
+    ("b1", 3, 3),
+    ("w4",),
+    ("b1", 2, 1),
+    ("b1", 1, 3),
+    ("b2", 0, 3),
+    ("b1", 1, 1),
+    ("b1", 0, 1),
+    ("b2", 2, 0),
+    ("b2", 3, 0),
+    ("b2", 0, 0),
     ("b2", 1, 2),
-    ("b1", 0, 2),
-    ("b1", 0, 1),
-    ("b0", 0, 3),
-    ("b2", 0, 0),
+    ("b1", 3, 1),
+    ("b2", 0, 2),
+    ("b2", 3, 2),
+    ("b2", 2, 2),
     ("b1", 2, 3),
-    ("b2", 2, 0),
+    ("b2", 1, 1),
     ("b2", 1, 3),
+    ("b2", 2, 1),
+    ("b2", 0, 1),
+    ("b2", 3, 3),
+    ("b2", 3, 1),
     ("w5",),
-    ("b2", 2, 2),
-    ("b2", 1, 1),
-    ("b1", 0, 3),
-    ("b2", 0, 2),
-    ("b2", 0, 1),
-    ("b2", 2, 1),
     ("b2", 2, 3),
+    ("b3", 2),
+    ("w6",),
     ("b3", 1),
-    ("b2", 0, 3),
-    ("w6",),
     ("b3", 0),
-    ("b3", 2),
+    ("b3", 3),
 )
 FAR = 1 << 17
-GROUPS = 41 * CHUNKS + 6 - len(DIRECT_SUMS) - len(DIRECT_SPREAD)
+GROUPS = 30 * CHUNKS + 6 - 2 * len(DIRECT_SUMS) - len(DIRECT_SPREAD)
 
 
 def wrap(value):
@@ -217,7 +246,7 @@
     pl.semaphore_wait(barrier, len(partners))
 
     def first_way(c):
-        return (1, -1, -1)[c]
+        return (1, -1, 1, -1)[c]
 
     def second_way(a):
         return 1 if a in (0, 1) else -1
@@ -226,10 +255,8 @@
         for h in range(2):
             src = G[c].at[at_k(h, a, 0)]
             for step in (1, -1):
-                side = "in" if step == second_way(a) else "by"
-                name = "all" if side == "by" and a in (1, -1) else a
                 send(
-                    ("g2" + side, c, name),
+                    ("g2in", c, a) if step == second_way(a) else ("g2", c),
                     src,
                     G[c].at[at_k(h, a, -step)],
                     along(h, False, step),
@@ -265,7 +292,7 @@
         take(("g2in", c, a), 2)
         for h in range(2):
             send(
-                ("g2r", c, "all" if a in (1, -1) else a),
+                ("g2", c),
                 G[c].at[at_k(h, a, -e)],
                 G[c].at[at_k(h, a, 2)],
                 along(h, False, e),
@@ -286,12 +313,7 @@
         second_relay(c, 2)
 
     def gather_8(c):
-        take(("g2by", c, 0), 2)
-        take(("g2by", c, "all"), 4)
-        take(("g2by", c, 2), 2)
-        take(("g2r", c, 0), 2)
-        take(("g2r", c, "all"), 4)
-        take(("g2r", c, 2), 2)
+        take(("g2", c), 16)
 
     def tables_0():
         rows_got.wait()
@@ -372,13 +394,13 @@
     def reduce_1(c):
         XS[c][0] = paired(c, 2).astype(BF16)
         if c in DIRECT_SUMS:
-            send(("cf", c), XS[c].at[0], XR[c].at[0], dev(dx=2))
+            send(("cr", c), XS[c].at[0], XR[c].at[0], dev(dx=2))
         else:
             for half in range(2):
                 lines = pl.ds(half * TILE, TILE)
                 send(("cf", c, half), XS[c].at[0, lines], XR[c].at[0, lines], dev(dx=turn))
         XS[c][1] = paired(c, 3).astype(BF16)
-        send(("cd", c), XS[c].at[1], XR[c].at[1], dev(dx=-turn))
+        send(("cr", c), XS[c].at[1], XR[c].at[1], dev(dx=-turn))
         if c in DIRECT_SUMS:
             XS[c][2] = paired(c, 1).astype(BF16)
             send(("cr", c), XS[c].at[2], XR[c].at[2], dev(dx=turn))
@@ -396,13 +418,9 @@
 
     def reduce_3(c):
         value = paired(c, 0)
-        take(("cd", c), 2)
-        value = value + XR[c][1].astype(F32)
-        take(("cr", c), 2)
-        value = value + XR[c][2].astype(F32)
-        if c in DIRECT_SUMS:
-            take(("cf", c), 2)
-            value = value + XR[c][0].astype(F32)
+        take(("cr", c), 6 if c in DIRECT_SUMS else 4)
+        for n in range(0 if c in DIRECT_SUMS else 1, 3):
+            value = value + XR[c][n].astype(F32)
         HD[:, STARTS[c] : STARTS[c] + WIDTHS[c]] = value.astype(BF16)
 
     def turn_blocks(part):
@@ -574,7 +592,7 @@
             send(("bf", c, i), SB[c].at[h, i, 0], SR[c].at[h, i, 0], along(h, False, e))
         for h in range(2):
             SB[c][h, i, 1] = sum_of(c, h, a, -e).astype(BF16)
-            send(("bd", c, i), SB[c].at[h, i, 1], SR[c].at[h, i, 1], along(h, False, -e))
+            send(("br", c, i), SB[c].at[h, i, 1], SR[c].at[h, i, 1], along(h, False, -e))
 
     def back_1(c, i):
         name = NAMES[i]
@@ -587,31 +605,36 @@
     def back_2(c, i):
         name = NAMES[i]
         e = first_way(c)
-        take(("bd", c, i), 2)
-        take(("br", c, i), 2)
-        if name == "relay":
+        take(("br", c, i), 4)
+        if name == "relay" and c not in DIRECT_LAST:
             take(("tf", c), 2)
         for h in range(2):
             value = sum_of(c, h, offset(c, name), 0) + SR[c][h, i, 1].astype(F32)
             value = value + SR[c][h, i, 2].astype(F32)
             if name == "far":
+                step = 2 if c in DIRECT_LAST else e
                 SB[c][h, 4, 0] = value.astype(BF16)
-                send(("tf", c), SB[c].at[h, 4, 0], SR[c].at[h, 4, 0], along(h, True, e))
+                send(("tf", c), SB[c].at[h, 4, 0], SR[c].at[h, 4, 0], along(h, True, step))
             elif name == "near":
                 SB[c][h, 4, 1] = value.astype(BF16)
-                send(("td", c), SB[c].at[h, 4, 1], SR[c].at[h, 4, 1], along(h, True, -e))
+                send(("tr", c), SB[c].at[h, 4, 1], SR[c].at[h, 4, 1], along(h, True, -e))
             elif name == "relay":
-                SB[c][h, 4, 2] = (value + SR[c][h, 4, 0].astype(F32)).astype(BF16)
+                if c not in DIRECT_LAST:
+                    value = value + SR[c][h, 4, 0].astype(F32)
+                SB[c][h, 4, 2] = value.astype(BF16)
                 send(("tr", c), SB[c].at[h, 4, 2], SR[c].at[h, 4, 2], along(h, True, e))
             else:
                 UK[c][h] = value
 
     def back_3(c):
-        take(("td", c), 2)
-        take(("tr", c), 2)
+        take(("tr", c), 4)
+        if c in DIRECT_LAST:
+            take(("tf", c), 2)
         for h in range(2):
             value = UK[c][h] + SR[c][h, 4, 1].astype(F32)
             value = value + SR[c][h, 4, 2].astype(F32)
+            if c in DIRECT_LAST:
+                value = value + SR[c][h, 4, 0].astype(F32)
             FO[h * TILE : (h + 1) * TILE, STARTS[c] : STARTS[c] + WIDTHS[c]] = value.astype(BF16)
 
     def multiply_back_all(c):

time: 79.4 us -> 77.6 us (0.977)
  Pallas kernels: 78 us -> 76.2 us
    pallas_call x1, Pallas kernels: 76.8 us -> 75.1 us  [shards(): pl.pallas_call(functools.partial(step_kernel, scale), out_shape=shapes, i...]
where the time goes in v5:
time: 77.6 us; the launch traced here: 77.5 us
  Pallas kernels  76.2 us (98%)
  between operations  1.29 us (2%)
    pallas_call x1, Pallas kernels, shards(): pl.pallas_call(functools.partial(step_kernel, scale), out_shape=shapes, i...  75.1 us

profile of v5, /device:TPU:0, one launch (start us, length us, event | category | flops | bytes accessed | tf_op | source)
XLA Modules:
  0.0 77.5 jit_solution(7997851540014229431)
XLA Ops:
  1.3 75.1 %graph_layer.1 = (bf16[256,512]{1,0:T(8,128)(2,1)S(1)}, bf16[256,512]{1,0:T(8,128)(2,1)S(1)}, f32[512,512]{1,0:T(8,128)S(1)}, f32[1,512]{1,0:T(1,128)S(1)}) custom-call(s32[1,1]{1,0:T(1,128)S(6)} %copy.12.count, s32[1,48]{1,0:T(1,128)} %bitcast.7, s32[1,48]{1,0:T(1,128)} %bitcast.8, bf16[256,512]{1,0:T(8,128)(2,1)} %feat.1, bf16[48,128,128]{2,1,0:T(8,128)(2,1)} %bitcast.5, ...), custom_call_target="tpu_custom_call" | custom-call | tf_op jit(solution)/shard_map/graph_layer/pallas_call | solution.py:679
  76.3 1.2 %finish.1 = (bf16[256,512]{1,0:T(8,128)(2,1)}, bf16[256,512]{1,0:T(8,128)(2,1)}, f32[512,512]{1,0:T(8,128)}, f32[1,512]{1,0:T(1,128)}) custom-call(bf16[256,512]{1,0:T(8,128)(2,1)S(1)} %get-tuple-element.12.a, bf16[256,512]{1,0:T(8,128)(2,1)S(1)} %get-tuple-element.13.b, f32[512,512]{1,0:T(8,128)S(1)} %get-tuple-element.14.c, f32[1,512]{1,0:T(1,128)S(1)} %get-tuple-element.15.d), custom_call_target="tpu_custom_call" | custom-call | tf_op jit(solution)/shard_map/finish/pallas_call | solution.py:738
